TPU v7x, 256 devices: a whole 4x4x8 slice. The times are simulated.
256 devices in a mesh: rows: 32 (over y, z), cols: 8 (over x, core).
Axes of the slice: x: 4, y: 4, z: 8, core: 2. Of those that a mesh axis runs over, the one named last changes fastest.
Arguments:
- orthophoto: float32 [3, 4096, 4096], P(None, 'rows', 'cols'), may hold values from 0 to 1
Outputs:
- detail_zero: float32 [3, 4096, 4096], P(None, 'rows', 'cols')
- detail_one: float32 [3, 2048, 2048], P(None, 'rows', 'cols')
- detail_two: float32 [3, 1024, 1024], P(None, 'rows', 'cols')
- detail_three: float32 [3, 512, 512], P(None, 'rows', 'cols')
- detail_four: float32 [3, 256, 256], P(None, 'rows', 'cols')
- coarsest: float32 [3, 128, 128], P(None, 'rows', 'cols')
All inputs are finite; a program needn't handle non-finite values.
Results may differ from a plain program's by a relative error of at most 0.00015.
Values sent between devices are 32-bit elements; how exact they have to be, the bound alone decides.
No kernel may reach another device: no remote copies, remote signals or barrier semaphores. Data moves between devices by JAX's collectives and lax.ppermute only.
A program may use at most 64 MiB of HBM per device.

v0:
```python
import functools

import jax
import jax.numpy as jnp
import ml_dtypes
import numpy as np
from jax import lax
from jax.experimental import pallas as pl
from jax.experimental.pallas import tpu as pltpu
from jax.sharding import PartitionSpec as P

LEVELS = 5
F32 = jnp.float32
BF16 = jnp.bfloat16


def reduce_matrix(n):
    pad = np.pad(np.arange(n), (2, 2), mode="reflect")
    out = np.zeros((n // 2, n))
    for j in range(n // 2):
        for s, w in enumerate((1, 4, 6, 4, 1)):
            out[j, pad[2 * j + s]] += w / 16
    return out


def levels_of(n):
    out, total = [], np.eye(n)
    for _ in range(LEVELS):
        total = reduce_matrix(total.shape[0]) @ total
        out.append(total)
    return out


def own_rows(n, which):
    big = levels_of(5 * n)
    out = []
    for level in big:
        m = level.shape[0] // 5
        out.append(np.stack([level[2 * m + j, 2 * n : 3 * n] for j in which(m)]))
    return out


def low_fix(n):
    big, out = levels_of(3 * n), []
    for level, own in zip(big, own_rows(n, lambda m: (-1, 0, 1))):
        assert not level[:2, n:].any()
        out.append(np.stack([level[1, :n], level[0, :n], level[1, :n]]) - own)
    return out


def high_fix(n):
    big, out = levels_of(3 * n), []
    for level, own in zip(big, own_rows(n, lambda m: (m - 1, m))):
        assert not level[-1, : 2 * n].any()
        out.append(np.stack([level[-1, 2 * n :]] * 2) - own)
    return out


def expand_matrix(m):
    out = np.zeros((2 * m, m + 2))
    for i in range(m):
        out[2 * i, i : i + 3] = (0.125, 0.75, 0.125)
        out[2 * i + 1, i + 1 : i + 3] = 0.5
    return out


def exact(matrix, pieces):
    out, rest = [], np.asarray(matrix, np.float64)
    for _ in range(pieces):
        part = rest.astype(ml_dtypes.bfloat16)
        out.append(part)
        rest = rest - part.astype(np.float64)
    assert not rest.any()
    return out


def put(rows, where, count):
    out = np.zeros((count, rows[0].shape[-1]))
    for row, at in zip(rows, where):
        out[at] = row
    return out


OWN_LANE = (0, 256, 384, 448, 480)
LOW_LANE = tuple(496 + k for k in range(LEVELS))
HIGH_LANE = tuple(501 + k for k in range(LEVELS))
ROWS = (72, 40, 24, 16, 8)
ROW_AT = (0, 72, 112, 136, 152)
ROWS_ALL = 160


@functools.lru_cache(None)
def constants(height, width):
    c = {}
    flat = lambda groups: np.concatenate(groups)
    left = flat(own_rows(width, lambda m: (-1, 0)))
    right = flat(own_rows(width, lambda m: (m - 1, m, m + 1)))
    low, high = flat(low_fix(width)), flat(high_fix(width))
    rows = np.zeros((64, width))
    rows[0:10], rows[16:31], rows[32:47], rows[48:58] = left, right, low, high
    c["edge"] = np.concatenate(exact(rows, 2))
    own = np.zeros((width, 512))
    parts = own_rows(width, lambda m: range(-1, m + 1))
    for k, part in enumerate(parts):
        m = part.shape[0] - 2
        own[:, OWN_LANE[k] : OWN_LANE[k] + m] = part[1:-1].T
        own[:, LOW_LANE[k]], own[:, HIGH_LANE[k]] = part[0], part[-1]
    c["col_a"] = exact(own[:, :384], 1)[0]
    c["col_b"] = np.concatenate(exact(own[:, 384:], 2), axis=1)
    land = np.zeros((32, 512))
    for k in range(LEVELS):
        m = width >> (k + 1)
        for q, at in enumerate((LOW_LANE[k], OWN_LANE[k], OWN_LANE[k] + 1)):
            land[3 * k + q, at] = 1
        for q, at in enumerate((OWN_LANE[k] + m - 1, HIGH_LANE[k])):
            land[16 + 2 * k + q, at] = 1
    c["col_land"] = exact(land, 1)[0]
    parts = own_rows(height, lambda m: range(-1, m + 1))
    level_rows = []
    for k, part in enumerate(parts):
        m = part.shape[0] - 2
        level_rows.append(put([*part[1:-1], part[0], part[-1]], range(m + 2), ROWS[k]))
    up, down = own_rows(height, lambda m: (-1, 0)), own_rows(height, lambda m: (m - 1, m, m + 1))
    low, high = low_fix(height), high_fix(height)
    c["row_1"] = exact(np.concatenate([level_rows[0], put([*down[0], *low[0], *up[0], *high[0]], range(10), 16)]), 1)[0]
    c["row_2"] = exact(np.concatenate([level_rows[1], put([*down[1], *low[1], *up[1], *high[1]], range(10), 16)]), 1)[0]
    ends = np.zeros((64, height))
    ends[0:15], ends[16:31], ends[32:42], ends[48:58] = flat(down), flat(low), flat(up), flat(high)
    c["row_3"] = np.concatenate(exact(np.concatenate([*level_rows, ends]), 2))
    land = np.zeros((ROWS_ALL, 48))
    for k in range(LEVELS):
        m = height >> (k + 1)
        for q, at in enumerate((m, 0, 1)):
            land[ROW_AT[k] + at, 3 * k + q] = 1
        for q, at in enumerate((m - 1, m + 1)):
            land[ROW_AT[k] + at, 32 + 2 * k + q] = 1
    c["row_land_3"] = exact(land, 1)[0]
    for name, k, tiles in (("row_land_1", 0, (0, 1)), ("row_land_2", 1, (2,))):
        m = height >> (k + 1)
        for t in tiles:
            land = np.zeros((ROWS[k], 48))
            for q, at in enumerate((m, 0, 1)):
                land[at, 16 + 3 * t + q] = 1
            for q, at in enumerate((m - 1, m + 1)):
                land[at, 42 + 2 * t + q] = 1
            c[f"{name}_{t}"] = exact(land, 1)[0]
    for k in range(LEVELS):
        m = width >> (k + 1)
        e = expand_matrix(m).T
        lanes = np.zeros((512, 2 * m))
        lanes[OWN_LANE[k] : OWN_LANE[k] + m] = e[1:-1]
        lanes[LOW_LANE[k]], lanes[HIGH_LANE[k]] = e[0], e[-1]
        if k == 0:
            lanes = np.concatenate([lanes[:256], lanes[384:]])
        else:
            lanes = lanes[256:] if k == 1 else lanes[384:]
        if k >= 3:
            at = OWN_LANE[k - 1] - 384
            wide = np.zeros((128, 128))
            wide[:, at : at + 2 * m] = lanes
            lanes = wide
        c[f"ecol_{k}"] = exact(lanes, 1)[0]
        m = height >> (k + 1)
        e = expand_matrix(m)
        c[f"erow_{k}"] = exact(np.concatenate([e[:, 1:-1], e[:, :1], e[:, -1:], np.zeros((2 * m, ROWS[k] - m - 2))], axis=1), 1)[0]
    return c


def split(x):
    high = x.astype(BF16)
    rest = x - high.astype(F32)
    middle = rest.astype(BF16)
    return high, middle, (rest - middle.astype(F32)).astype(BF16)


def times(x, matrix):
    return sum(jnp.dot(part, matrix, preferred_element_type=F32) for part in split(x))


def times_left(matrix, x):
    return sum(jnp.dot(matrix, part, preferred_element_type=F32) for part in split(x))


def edge_kernel(x_ref, edge_ref, left_ref, right_ref, low_ref, high_ref):
    for ch in range(x_ref.shape[0]):
        both = sum(
            lax.dot_general(edge_ref[...], part, (((1,), (1,)), ((), ())), preferred_element_type=F32)
            for part in split(x_ref[ch])
        )
        rows = both[:64] + both[64:]
        left_ref[ch], right_ref[ch], low_ref[ch], high_ref[ch] = rows[:16], rows[16:32], rows[32:48], rows[48:]


def column_kernel(x_ref, a_ref, b_ref, u_ref):
    for ch in range(x_ref.shape[0]):
        parts = split(x_ref[ch])
        u_ref[ch, :, :384] = sum(jnp.dot(p, a_ref[...], preferred_element_type=F32) for p in parts)
        last = sum(jnp.dot(p, b_ref[...], preferred_element_type=F32) for p in parts)
        u_ref[ch, :, 384:] = last[:, :128] + last[:, 128:]


def row_kernel(
    u_ref, from_left_ref, from_right_ref, low_ref, high_ref, land_ref, r1_ref, r2_ref, r3_ref,
    t1_ref, t2_ref, t3_ref, down_ref, up_ref, first_ref, last_ref,
):
    col = lax.axis_index("cols")
    is_first, is_last = col == 0, col == lax.axis_size("cols") - 1
    down_ref[...] = jnp.zeros_like(down_ref)
    first_ref[...] = jnp.zeros_like(first_ref)
    for ch in range(u_ref.shape[0]):
        got = jnp.concatenate(
            [
                jnp.where(is_first, low_ref[ch], from_left_ref[ch]),
                jnp.where(is_last, high_ref[ch], from_right_ref[ch]),
            ],
            axis=0,
        )
        v = u_ref[ch] + times(got.T, land_ref[...])
        n1, n2 = ROWS[0], ROWS[1]
        one = times_left(r1_ref[...], v[:, :256])
        two = times_left(r2_ref[...], v[:, 256:384])
        both = times_left(r3_ref[...], v[:, 384:])
        three = both[: ROWS_ALL + 64] + both[ROWS_ALL + 64 :]
        t1_ref[ch] = one[:n1]
        t2_ref[ch] = two[:n2]
        t3_ref[ch] = three[:ROWS_ALL]
        ends = three[ROWS_ALL:]
        for ref, base, at in ((down_ref, 0, 0), (first_ref, 16, 3)):
            ref[ch, 0:16] = ends[base : base + 16]
            ref[ch, 16:19] = one[n1 + at : n1 + at + 3, :128]
            ref[ch, 19:22] = one[n1 + at : n1 + at + 3, 128:]
            ref[ch, 22:25] = two[n2 + at : n2 + at + 3]
        for ref, base, at in ((up_ref, 32, 6), (last_ref, 48, 8)):
            ref[ch, 0:10] = ends[base : base + 10]
            ref[ch, 10:12] = one[n1 + at : n1 + at + 2, :128]
            ref[ch, 12:14] = one[n1 + at : n1 + at + 2, 128:]
            ref[ch, 14:16] = two[n2 + at : n2 + at + 2]


def detail_kernel(
    x_ref, t1_ref, t2_ref, t3_ref, from_up_ref, from_down_ref, first_ref, last_ref,
    l10_ref, l11_ref, l22_ref, l3_ref, ec0, ec1, ec2, ec3, ec4, er0, er1, er2, er3, er4,
    d0_ref, d1_ref, d2_ref, d3_ref, d4_ref, coarsest_ref,
):
    row = lax.axis_index("rows")
    is_first, is_last = row == 0, row == lax.axis_size("rows") - 1
    for ch in range(x_ref.shape[0]):
        got = jnp.concatenate(
            [
                jnp.where(is_first, first_ref[ch], from_up_ref[ch]),
                jnp.where(is_last, last_ref[ch], from_down_ref[ch]),
            ],
            axis=0,
        )
        one = jnp.concatenate(
            [
                t1_ref[ch, :, :128] + times_left(l10_ref[...], got),
                t1_ref[ch, :, 128:] + times_left(l11_ref[...], got),
            ],
            axis=1,
        )
        two = t2_ref[ch] + times_left(l22_ref[...], got)
        three = t3_ref[ch] + times_left(l3_ref[...], got)
        lv = [three[ROW_AT[k] : ROW_AT[k] + ROWS[k]] for k in range(LEVELS)]
        e = times_left(er0[...], times(jnp.concatenate([one, lv[0]], axis=1), ec0[...]))
        d0_ref[ch] = x_ref[ch] - e
        e = times_left(er1[...], times(jnp.concatenate([two, lv[1]], axis=1), ec1[...]))
        d1_ref[ch] = one[: e.shape[0]] - e
        e = times_left(er2[...], times(lv[2], ec2[...]))
        d2_ref[ch] = two[: e.shape[0]] - e
        e = times_left(er3[...], times(lv[3], ec3[...]))
        d3_ref[ch] = (lv[2][: e.shape[0]] - e)[:, :64]
        e = times_left(er4[...], times(lv[4], ec4[...]))
        d4_ref[ch] = (lv[3][: e.shape[0]] - e)[:, 64:96]
        coarsest_ref[ch] = lv[4][:4, 96:112]


def call(kernel, outs, flops, *args):
    bytes_of = lambda a: a.size * a.dtype.itemsize
    outs = [jax.ShapeDtypeStruct(s, F32) for s in outs]
    return pl.pallas_call(
        kernel,
        out_shape=outs,
        in_specs=[pl.BlockSpec(memory_space=pltpu.VMEM)] * len(args),
        out_specs=[pl.BlockSpec(memory_space=pltpu.VMEM)] * len(outs),
        compiler_params=pltpu.CompilerParams(vmem_limit_bytes=24 * 2**20),
        cost_estimate=pl.CostEstimate(
            flops=flops, bytes_accessed=sum(bytes_of(a) for a in args), transcendentals=0
        ),
    )(*args)


def shift(x, axis, step):
    count = lax.axis_size(axis)
    pairs = [(i, i + step) for i in range(count) if 0 <= i + step < count]
    return lax.ppermute(x, axis, pairs)


def body(x):
    channels, height, width = x.shape
    c = {name: jnp.asarray(value) for name, value in constants(height, width).items()}
    side = (channels, 16, height)
    left, right, low, high = call(edge_kernel, [side] * 4, 10**8, x, c["edge"])
    from_left = shift(right, "cols", 1)
    from_right = shift(left, "cols", -1)
    (u,) = call(column_kernel, [(channels, height, 512)], 10**9, x, c["col_a"], c["col_b"])
    t1, t2, t3, down, up, first, last = call(
        row_kernel,
        [(channels, ROWS[0], 256), (channels, ROWS[1], 128), (channels, ROWS_ALL, 128)]
        + [(channels, 32, 128), (channels, 16, 128)] * 2,
        10**8,
        u, from_left, from_right, low, high, c["col_land"], c["row_1"], c["row_2"], c["row_3"],
    )
    from_up = shift(down, "rows", 1)
    from_down = shift(up, "rows", -1)
    outs = [(channels, height >> k, width >> k) for k in range(LEVELS + 1)]
    return call(
        detail_kernel, outs, 10**9,
        x, t1, t2, t3, from_up, from_down, first, last,
        c["row_land_1_0"], c["row_land_1_1"], c["row_land_2_2"], c["row_land_3"],
        *(c[f"ecol_{k}"] for k in range(LEVELS)), *(c[f"erow_{k}"] for k in range(LEVELS)),
    )


def solution(mesh):
    placed = P(None, "rows", "cols")
    return jax.shard_map(
        body, mesh=mesh, in_specs=(placed,), out_specs=(placed,) * 6, check_vma=False
    )
```

profile of v0, /device:TPU:117, one launch (start us, length us, event | category | flops | bytes accessed | tf_op | source)
XLA Modules:
  0.0 29.1 jit_solution(18085955138297590540)
XLA Ops:
  0.6 1.1 %copy-done = f32[3,128,512]{2,1,0:T(8,128)S(1)} copy-done((f32[3,128,512]{2,1,0:T(8,128)S(1)}, f32[3,128,512]{2,1,0:T(8,128)}, u32[]{:S(2)}) %copy-start) | copy-done | bytes 786456
  1.8 0.9 %copy-done.2 = bf16[128,512]{1,0:T(8,128)(2,1)S(1)} copy-done((bf16[128,512]{1,0:T(8,128)(2,1)S(1)}, bf16[128,512]{1,0:T(8,128)(2,1)}, u32[]{:S(2)}) %copy-start.2) | copy-done | bytes 131096
  2.7 0.5 %shard_map.254 = (f32[3,16,128]{2,1,0:T(8,128)S(1)}, f32[3,16,128]{2,1,0:T(8,128)S(1)}, f32[3,16,128]{2,1,0:T(8,128)S(1)}, f32[3,16,128]{2,1,0:T(8,128)S(1)}) custom-call(f32[3,128,512]{2,1,0:T(8,128)S(1)} %copy-done, bf16[128,512]{1,0:T(8,128)(2,1)S(1)} %copy-done.2), custom_call_target="tpu_custom_call" | custom-call | flops 100000000 | bytes 917504 | tf_op jit(solution)/shard_map/pallas_call | solution.py:281
  3.2 3.4 %collective-permute-start = (f32[3,16,128]{2,1,0:T(8,128)S(1)}, f32[3,16,128]{2,1,0:T(8,128)S(1)}, u32[]{:S(2)}, u32[]{:S(2)}) collective-permute-start(f32[3,16,128]{2,1,0:T(8,128)S(1)} %get-tuple-element.17), channel_id=1, source_target_pairs={{0,1},{1,2},{2,3},{3,4},{4,5},{5,6},{6,7},{8,9},{9,10},{10,11},{11... | collective-permute-start | bytes 73736 | tf_op jit(solution)/shard_map/ppermute | solution.py:296
  6.5 0.0 copy-start.3
  6.6 0.0 copy-start.4
  6.6 0.0 copy-start.5
  6.6 2.1 %collective-permute-start.1 = (f32[3,16,128]{2,1,0:T(8,128)S(1)}, f32[3,16,128]{2,1,0:T(8,128)S(1)}, u32[]{:S(2)}, u32[]{:S(2)}) collective-permute-start(f32[3,16,128]{2,1,0:T(8,128)S(1)} %get-tuple-element.18), channel_id=1, source_target_pairs={{1,0},{2,1},{3,2},{4,3},{5,4},{6,5},{7,6},{9,8},{10,9},{11,10},{12... | collective-permute-start | bytes 73736 | tf_op jit(solution)/shard_map/ppermute | solution.py:296
  8.7 0.0 copy-start.7
  8.7 0.0 copy-start.15
  8.7 0.0 copy-start.17
  8.7 0.0 copy-start.18
  8.7 0.0 copy-start.21
  8.8 0.0 copy-start.22
  8.8 1.1 %shard_map.253.u_ref = f32[3,128,512]{2,1,0:T(8,128)S(1)} custom-call(f32[3,128,512]{2,1,0:T(8,128)S(1)} %copy-done, bf16[512,384]{1,0:T(8,128)(2,1)S(1)} %copy-done.8, bf16[512,256]{1,0:T(8,128)(2,1)S(1)} %copy-done.9), custom_call_target="tpu_custom_call" | custom-call | flops 1000000000 | bytes 1441792 | tf_op jit(solution)/shard_map/pallas_call | solution.py:281
  9.9 1.9 %collective-permute-done.1.from_right_ref = f32[3,16,128]{2,1,0:T(8,128)S(1)} collective-permute-done((f32[3,16,128]{2,1,0:T(8,128)S(1)}, f32[3,16,128]{2,1,0:T(8,128)S(1)}, u32[]{:S(2)}, u32[]{:S(2)}) %collective-permute-start.1) | collective-permute-done | bytes 24608 | tf_op jit(solution)/shard_map/ppermute | solution.py:296
  11.9 0.0 copy-start.10
  11.9 0.0 copy-start.11
  11.9 0.0 copy-start.12
  12.0 1.5 %shard_map.255 = (f32[3,72,256]{2,1,0:T(8,128)S(1)}, f32[3,40,128]{2,1,0:T(8,128)S(1)}, f32[3,160,128]{2,1,0:T(8,128)S(1)}, f32[3,32,128]{2,1,0:T(8,128)S(1)}, f...) custom-call(f32[3,128,512]{2,1,0:T(8,128)S(1)} %shard_map.253.u_ref, ...), custom_call_target="tpu_custom_call" | custom-call | flops 100000000 | bytes 1069056 | tf_op jit(solution)/shard_map/pallas_call | solution.py:281
  13.5 4.8 %collective-permute-start.2 = (f32[3,32,128]{2,1,0:T(8,128)S(1)}, f32[3,32,128]{2,1,0:T(8,128)S(1)}, u32[]{:S(2)}, u32[]{:S(2)}) collective-permute-start(f32[3,32,128]{2,1,0:T(8,128)S(1)} %get-tuple-element.24), channel_id=1, source_target_pairs={{0,8},{8,16},{16,24},{24,32},{32,40},{40,48},{48,56},{56,64},{64,7... | collective-permute-start | bytes 147464 | tf_op jit(solution)/shard_map/ppermute | solution.py:296
  18.3 1.9 %collective-permute-start.3 = (f32[3,16,128]{2,1,0:T(8,128)S(1)}, f32[3,16,128]{2,1,0:T(8,128)S(1)}, u32[]{:S(2)}, u32[]{:S(2)}) collective-permute-start(f32[3,16,128]{2,1,0:T(8,128)S(1)} %get-tuple-element.25), channel_id=1, source_target_pairs={{8,0},{16,8},{24,16},{32,24},{40,32},{48,40},{56,48},{64,56},{72,6... | collective-permute-start | bytes 73736 | tf_op jit(solution)/shard_map/ppermute | solution.py:296
  20.2 4.3 %collective-permute-done.3.from_down_ref = f32[3,16,128]{2,1,0:T(8,128)S(1)} collective-permute-done((f32[3,16,128]{2,1,0:T(8,128)S(1)}, f32[3,16,128]{2,1,0:T(8,128)S(1)}, u32[]{:S(2)}, u32[]{:S(2)}) %collective-permute-start.3) | collective-permute-done | bytes 24608 | tf_op jit(solution)/shard_map/ppermute | solution.py:296
  24.6 4.5 %shard_map.256 = (f32[3,128,512]{2,1,0:T(8,128)}, f32[3,64,256]{2,1,0:T(8,128)}, f32[3,32,128]{2,1,0:T(8,128)}, f32[3,16,64]{2,1,0:T(8,128)}, f32[3,8,32]{2,1,0:T(8,128)}, /*index=5*/f32[3,4,16]{2,1,0:T(4,128)}) custom-call(f32[3,128,512]{2,1,0:T(8,128)S(1)} %copy-done.1, f32[3,72,256]{2,1,0:T(8,128)S(1)} %get-tuple-element.21.t1_ref, ...), custom_call_target="tpu_custom_call" | custom-call | flops 1000000000 | bytes 2143616 | tf_op jit(solution)/shard_map/pallas_call | solution.py:281
  (34 shorter events, 0.1 us)
Async XLA Ops:
  2.7 6.0 %copy-start.8 = (bf16[512,384]{1,0:T(8,128)(2,1)S(1)}, bf16[512,384]{1,0:T(8,128)(2,1)}, u32[]{:S(2)}) copy-start(bf16[512,384]{1,0:T(8,128)(2,1)} %constant.43.clone.a_ref) | copy-start | bytes 1179652
  2.7 6.0 %copy-start.9 = (bf16[512,256]{1,0:T(8,128)(2,1)S(1)}, bf16[512,256]{1,0:T(8,128)(2,1)}, u32[]{:S(2)}) copy-start(bf16[512,256]{1,0:T(8,128)(2,1)} %constant.44.clone.b_ref) | copy-start | bytes 786436
  3.2 6.8 %collective-permute-start = (f32[3,16,128]{2,1,0:T(8,128)S(1)}, f32[3,16,128]{2,1,0:T(8,128)S(1)}, u32[]{:S(2)}, u32[]{:S(2)}) collective-permute-start(f32[3,16,128]{2,1,0:T(8,128)S(1)} %get-tuple-element.17), channel_id=1, source_target_pairs={{0,1},{1,2},{2,3},{3,4},{4,5},{5,6},{6,7},{8,9},{9,10},{10,11},{11... | collective-permute-start | bytes 73736 | tf_op jit(solution)/shard_map/ppermute | solution.py:296
  6.5 5.3 %copy-start.3 = (bf16[448,128]{1,0:T(8,128)(2,1)S(1)}, bf16[448,128]{1,0:T(8,128)(2,1)}, u32[]{:S(2)}) copy-start(bf16[448,128]{1,0:T(8,128)(2,1)} %constant.48.clone.r3_ref) | copy-start | bytes 344068
  6.6 5.3 %copy-start.4 = (bf16[32,512]{1,0:T(8,128)(2,1)S(1)}, bf16[32,512]{1,0:T(8,128)(2,1)}, u32[]{:S(2)}) copy-start(bf16[32,512]{1,0:T(8,128)(2,1)} %constant.45.clone.land_ref) | copy-start | bytes 98308
  6.6 5.3 %copy-start.5 = (bf16[88,128]{1,0:T(8,128)(2,1)S(1)}, bf16[88,128]{1,0:T(8,128)(2,1)}, u32[]{:S(2)}) copy-start(bf16[88,128]{1,0:T(8,128)(2,1)} %constant.46.clone.r1_ref) | copy-start | bytes 67588
  6.6 5.3 %collective-permute-start.1 = (f32[3,16,128]{2,1,0:T(8,128)S(1)}, f32[3,16,128]{2,1,0:T(8,128)S(1)}, u32[]{:S(2)}, u32[]{:S(2)}) collective-permute-start(f32[3,16,128]{2,1,0:T(8,128)S(1)} %get-tuple-element.18), channel_id=1, source_target_pairs={{1,0},{2,1},{3,2},{4,3},{5,4},{6,5},{7,6},{9,8},{10,9},{11,10},{12... | collective-permute-start | bytes 73736 | tf_op jit(solution)/shard_map/ppermute | solution.py:296
  8.7 15.8 %copy-start.7 = (bf16[384,512]{1,0:T(8,128)(2,1)S(1)}, bf16[384,512]{1,0:T(8,128)(2,1)}, u32[]{:S(2)}) copy-start(bf16[384,512]{1,0:T(8,128)(2,1)} %constant.53.clone.ec0) | copy-start | bytes 1179652
  8.7 15.8 %copy-start.15 = (bf16[128,72]{1,0:T(8,128)(2,1)S(1)}, bf16[128,72]{1,0:T(8,128)(2,1)}, u32[]{:S(2)}) copy-start(bf16[128,72]{1,0:T(8,128)(2,1)} %constant.54.clone.er0) | copy-start | bytes 55300
  8.7 15.8 %copy-start.17 = (bf16[72,48]{1,0:T(8,128)(2,1)S(1)}, bf16[72,48]{1,0:T(8,128)(2,1)}, u32[]{:S(2)}) copy-start(bf16[72,48]{1,0:T(8,128)(2,1)} %constant.50.clone.l10_ref) | copy-start | bytes 20740
  8.7 15.8 %copy-start.18 = (bf16[64,40]{1,0:T(8,128)(2,1)S(1)}, bf16[64,40]{1,0:T(8,128)(2,1)}, u32[]{:S(2)}) copy-start(bf16[64,40]{1,0:T(8,128)(2,1)} %constant.56.clone.er1) | copy-start | bytes 15364
  8.7 15.8 %copy-start.20 = (bf16[32,24]{1,0:T(8,128)(2,1)S(1)}, bf16[32,24]{1,0:T(8,128)(2,1)}, u32[]{:S(2)}) copy-start(bf16[32,24]{1,0:T(8,128)(2,1)} %constant.58.clone.er2) | copy-start | bytes 4612
  8.7 15.8 %copy-start.21 = (bf16[16,16]{1,0:T(8,128)(2,1)S(1)}, bf16[16,16]{1,0:T(8,128)(2,1)}, u32[]{:S(2)}) copy-start(bf16[16,16]{1,0:T(8,128)(2,1)} %constant.60.clone.er3) | copy-start | bytes 1540
  8.8 15.8 %copy-start.22 = (bf16[8,8]{1,0:T(8,128)(2,1)S(1)}, bf16[8,8]{1,0:T(8,128)(2,1)}, u32[]{:S(2)}) copy-start(bf16[8,8]{1,0:T(8,128)(2,1)} %constant.62.clone.er4) | copy-start | bytes 388
  9.9 14.7 %copy-start.1 = (f32[3,128,512]{2,1,0:T(8,128)S(1)}, f32[3,128,512]{2,1,0:T(8,128)}, u32[]{:S(2)}) copy-start(f32[3,128,512]{2,1,0:T(8,128)} %x_ref.5) | copy-start | bytes 2359300
  11.9 12.7 %copy-start.10 = (bf16[256,256]{1,0:T(8,128)(2,1)S(1)}, bf16[256,256]{1,0:T(8,128)(2,1)}, u32[]{:S(2)}) copy-start(bf16[256,256]{1,0:T(8,128)(2,1)} %constant.55.clone.ec1) | copy-start | bytes 393220
  11.9 12.7 %copy-start.11 = (bf16[160,48]{1,0:T(8,128)(2,1)S(1)}, bf16[160,48]{1,0:T(8,128)(2,1)}, u32[]{:S(2)}) copy-start(bf16[160,48]{1,0:T(8,128)(2,1)} %constant.49.clone.l3_ref) | copy-start | bytes 46084
  11.9 12.7 %copy-start.12 = (bf16[128,128]{1,0:T(8,128)(2,1)S(1)}, bf16[128,128]{1,0:T(8,128)(2,1)}, u32[]{:S(2)}) copy-start(bf16[128,128]{1,0:T(8,128)(2,1)} %constant.61.clone.ec4) | copy-start | bytes 98308
  11.9 12.7 %copy-start.13 = (bf16[128,128]{1,0:T(8,128)(2,1)S(1)}, bf16[128,128]{1,0:T(8,128)(2,1)}, u32[]{:S(2)}) copy-start(bf16[128,128]{1,0:T(8,128)(2,1)} %constant.59.clone.ec3) | copy-start | bytes 98308
  11.9 12.7 %copy-start.14 = (bf16[128,128]{1,0:T(8,128)(2,1)S(1)}, bf16[128,128]{1,0:T(8,128)(2,1)}, u32[]{:S(2)}) copy-start(bf16[128,128]{1,0:T(8,128)(2,1)} %constant.57.clone.ec2) | copy-start | bytes 98308
  12.0 12.7 %copy-start.16 = (bf16[72,48]{1,0:T(8,128)(2,1)S(1)}, bf16[72,48]{1,0:T(8,128)(2,1)}, u32[]{:S(2)}) copy-start(bf16[72,48]{1,0:T(8,128)(2,1)} %constant.51.clone.l11_ref) | copy-start | bytes 20740
  13.5 11.1 %copy-start.19 = (bf16[40,48]{1,0:T(8,128)(2,1)S(1)}, bf16[40,48]{1,0:T(8,128)(2,1)}, u32[]{:S(2)}) copy-start(bf16[40,48]{1,0:T(8,128)(2,1)} %constant.52.clone.l22_ref) | copy-start | bytes 11524
  13.5 11.0 %collective-permute-start.2 = (f32[3,32,128]{2,1,0:T(8,128)S(1)}, f32[3,32,128]{2,1,0:T(8,128)S(1)}, u32[]{:S(2)}, u32[]{:S(2)}) collective-permute-start(f32[3,32,128]{2,1,0:T(8,128)S(1)} %get-tuple-element.24), channel_id=1, source_target_pairs={{0,8},{8,16},{16,24},{24,32},{32,40},{40,48},{48,56},{56,64},{64,7... | collective-permute-start | bytes 147464 | tf_op jit(solution)/shard_map/ppermute | solution.py:296
  18.3 6.2 %collective-permute-start.3 = (f32[3,16,128]{2,1,0:T(8,128)S(1)}, f32[3,16,128]{2,1,0:T(8,128)S(1)}, u32[]{:S(2)}, u32[]{:S(2)}) collective-permute-start(f32[3,16,128]{2,1,0:T(8,128)S(1)} %get-tuple-element.25), channel_id=1, source_target_pairs={{8,0},{16,8},{24,16},{32,24},{40,32},{48,40},{56,48},{64,56},{72,6... | collective-permute-start | bytes 73736 | tf_op jit(solution)/shard_map/ppermute | solution.py:296
  (3 other events, 7.3 us)
where the time goes:
time: 29.4 us; the launch traced here: 29.1 us
  starting transfers between devices  12.1 us (41%)
  Pallas kernels  7.59 us (26%)
  waiting for transfers between devices  6.26 us (21%)
  local copies, waits for them, and re-layouts  2.17 us (7%)
  between operations  0.99 us (3%)
    ppermute x4, starting transfers between devices, shift(): return lax.ppermute(x, axis, pairs)  12.1 us
    pallas_call x4, Pallas kernels, call(): pl.pallas_call(kernel, out_shape=outs, in_specs=[pl.BlockSpec(memory_spac...  7.59 us
    ppermute x4, waiting for transfers between devices, shift(): return lax.ppermute(x, axis, pairs)  6.26 us
    unnamed x46, local copies, waits for them, and re-layouts  2.17 us
  transfers between devices with their start and end apart: 4, of which 2 were waited for; matrix products, arithmetic and copies ran while one was open for 0% of the time, Pallas kernels for 4%

commit v1 on v0

v1 whole, which is shorter than its diff:
```python
import functools

import jax
import jax.numpy as jnp
import ml_dtypes
import numpy as np
from jax import lax
from jax.experimental import pallas as pl
from jax.experimental.pallas import tpu as pltpu
from jax.sharding import PartitionSpec as P

LEVELS = 5
F32 = jnp.float32
BF16 = jnp.bfloat16


def reduce_matrix(n):
    pad = np.pad(np.arange(n), (2, 2), mode="reflect")
    out = np.zeros((n // 2, n))
    for j in range(n // 2):
        for s, w in enumerate((1, 4, 6, 4, 1)):
            out[j, pad[2 * j + s]] += w / 16
    return out


def levels_of(n):
    out, total = [], np.eye(n)
    for _ in range(LEVELS):
        total = reduce_matrix(total.shape[0]) @ total
        out.append(total)
    return out


def own_rows(n, which):
    big = levels_of(5 * n)
    out = []
    for level in big:
        m = level.shape[0] // 5
        out.append(np.stack([level[2 * m + j, 2 * n : 3 * n] for j in which(m)]))
    return out


def low_fix(n):
    big, out = levels_of(3 * n), []
    for level, own in zip(big, own_rows(n, lambda m: (-1, 0, 1))):
        assert not level[:2, n:].any()
        out.append(np.stack([level[1, :n], level[0, :n], level[1, :n]]) - own)
    return out


def high_fix(n):
    big, out = levels_of(3 * n), []
    for level, own in zip(big, own_rows(n, lambda m: (m - 1, m))):
        assert not level[-1, : 2 * n].any()
        out.append(np.stack([level[-1, 2 * n :]] * 2) - own)
    return out


def expand_matrix(m):
    out = np.zeros((2 * m, m + 2))
    for i in range(m):
        out[2 * i, i : i + 3] = (0.125, 0.75, 0.125)
        out[2 * i + 1, i + 1 : i + 3] = 0.5
    return out


def exact(matrix, pieces):
    out, rest = [], np.asarray(matrix, np.float64)
    for _ in range(pieces):
        part = rest.astype(ml_dtypes.bfloat16)
        out.append(part)
        rest = rest - part.astype(np.float64)
    assert not rest.any()
    return out


OWN_LANE = (0, 256, 384, 448, 480)
LOW_LANE = tuple(496 + k for k in range(LEVELS))
HIGH_LANE = tuple(501 + k for k in range(LEVELS))
TILES = ((0, 1, 3), (2, 3), (3,), (3,), (3,))
TILE_LEVELS = (1, 1, 2, 5)
LEAD = 24
TAIL = 32


def rows_of(n):
    return -(-(n + 16) // 8) * 8


@functools.lru_cache(None)
def constants(width):
    c = {}
    left = np.concatenate(own_rows(width, lambda m: (-1, 0)))
    right = np.concatenate(own_rows(width, lambda m: (m - 1, m, m + 1)))
    low, high = np.concatenate(low_fix(width)), np.concatenate(high_fix(width))
    edge = np.zeros((2, 32, 128))
    for side, at, part in ((0, 0, left), (0, 16, low), (1, 0, right), (1, 16, high)):
        near, far = (part[:, :128], part[:, 128:]) if side == 0 else (part[:, -128:], part[:, :-128])
        assert not far.any()
        edge[side, at : at + len(part)] = near
    c["edge"] = np.concatenate(exact(edge, 2), axis=1)
    own = np.zeros((width, 512))
    for k, part in enumerate(own_rows(width, lambda m: range(-1, m + 1))):
        m = part.shape[0] - 2
        own[:, OWN_LANE[k] : OWN_LANE[k] + m] = part[1:-1].T
        own[:, LOW_LANE[k]], own[:, HIGH_LANE[k]] = part[0], part[-1]
    c["col_a"] = exact(own[:, :384], 1)[0]
    c["col_b"] = np.concatenate(exact(own[:, 384:], 2), axis=1)
    land = np.zeros((32, 512))
    for k in range(LEVELS):
        m = width >> (k + 1)
        for q, at in enumerate((LOW_LANE[k], OWN_LANE[k], OWN_LANE[k] + 1)):
            land[3 * k + q, at] = 1
        for q, at in enumerate((OWN_LANE[k] + m - 1, HIGH_LANE[k])):
            land[16 + 2 * k + q, at] = 1
    c["land"] = exact(land, 1)[0]
    for k in range(LEVELS):
        m = width >> (k + 1)
        e = expand_matrix(m).T
        lanes = np.zeros((512, 2 * m))
        lanes[OWN_LANE[k] : OWN_LANE[k] + m] = e[1:-1]
        lanes[LOW_LANE[k]], lanes[HIGH_LANE[k]] = e[0], e[-1]
        if k == 0:
            lanes = np.concatenate([lanes[:256], lanes[384:]])
        else:
            lanes = lanes[256:] if k == 1 else lanes[384:]
        if k >= 3:
            at = OWN_LANE[k - 1] - 384
            wide = np.zeros((128, 128))
            wide[:, at : at + 2 * m] = lanes
            lanes = wide
        c[f"expand_{k}"] = exact(lanes, 1)[0]
    return c


def split(x):
    high = x.astype(BF16)
    rest = x - high.astype(F32)
    middle = rest.astype(BF16)
    return [high, middle, (rest - middle.astype(F32)).astype(BF16)]


def times(x, matrix):
    rows = x.shape[0]
    out = jnp.dot(jnp.concatenate(split(x), axis=0), matrix, preferred_element_type=F32)
    return out[:rows] + out[rows : 2 * rows] + out[2 * rows :]


def edge_kernel(
    x_hbm, edge_hbm, a_hbm, b_hbm, land_hbm,
    send_b_ref, send_a_ref, low_ref, high_ref, x_ref, a_ref, b_ref, land_ref,
    edge_ref, sems,
):
    channels, height, width = x_hbm.shape
    lanes = [pl.ds(0, 128), pl.ds(width - 128, 128), pl.ds(128, width - 256)]
    pairs = [(edge_hbm, edge_ref)] + [(x_hbm.at[:, :, at], x_ref.at[:, :, at]) for at in lanes]
    pairs += [(a_hbm, a_ref), (b_hbm, b_ref), (land_hbm, land_ref)]
    copies = [pltpu.make_async_copy(source, target, sems.at[i]) for i, (source, target) in enumerate(pairs)]
    for copy in copies:
        copy.start()
    for copy in copies[:3]:
        copy.wait()
    odd = lax.axis_index("cols") % 2 == 1
    sides = []
    for side in range(2):
        out = sum(
            lax.dot_general(edge_ref[side], part, (((1,), (1,)), ((), ())), preferred_element_type=F32)
            for part in split(x_ref[:, :, lanes[side].start : lanes[side].start + 128].reshape(channels * height, 128))
        )
        sides.append(out[:32] + out[32:])
    left, right = sides
    for ch in range(channels):
        at = slice(ch * height, (ch + 1) * height)
        send_b_ref[ch] = jnp.where(odd, right[:16, at], left[:16, at])
        send_a_ref[ch] = jnp.where(odd, left[:16, at], right[:16, at])
        low_ref[ch], high_ref[ch] = left[16:, at], right[16:, at]
    for copy in copies[3:]:
        copy.wait()


def column_kernel(x_ref, a_ref, b_ref, u_ref):
    channels, height, width = x_ref.shape
    x = x_ref[...].reshape(channels * height, width)
    u_ref[:, :, :384] = times(x, a_ref[...]).reshape(channels, height, 384)
    last = times(x, b_ref[...])
    u_ref[:, :, 384:] = (last[:, :128] + last[:, 128:]).reshape(channels, height, 128)


def with_row(rows, at, when, new):
    index = lax.broadcasted_iota(jnp.int32, rows.shape, 1)
    return jnp.where((index == at) & when, new, rows)


def row_kernel(
    u_ref, got_b_ref, got_a_ref, low_ref, high_ref, land_ref,
    t1_ref, t2_ref, t3_ref, t4_ref, t5_ref, down_ref, up_ref,
    v_ref, c1_ref, c2_ref, c3_ref, c4_ref,
):
    channels, height = u_ref.shape[0], u_ref.shape[1]
    col, row = lax.axis_index("cols"), lax.axis_index("rows")
    col_odd = col % 2 == 1
    first, last = row == 0, row == lax.axis_size("rows") - 1
    got = []
    for ch in range(channels):
        b, a = got_b_ref[ch], got_a_ref[ch]
        from_left = jnp.where(col == 0, low_ref[ch], jnp.where(col_odd, a, b))
        from_right = jnp.where(col == lax.axis_size("cols") - 1, high_ref[ch], jnp.where(col_odd, b, a))
        got.append(jnp.concatenate([from_left, from_right], axis=0).T)
    landed = times(jnp.concatenate(got, axis=0), land_ref[...])
    chain = (v_ref, c1_ref, c2_ref, c3_ref, c4_ref)
    for k, ref in enumerate(chain):
        n = height >> k
        tiles, size = ref.shape[0], ref.shape[1]
        ref[:, :LEAD] = jnp.zeros((tiles, LEAD, 128), F32)
        ref[:, LEAD + n :] = jnp.zeros((tiles, size - LEAD - n, 128), F32)
    for ch in range(channels):
        for t in range(4):
            lanes = slice(128 * t, 128 * (t + 1))
            v_ref[4 * ch + t, LEAD : LEAD + height] = (
                u_ref[ch, :, lanes] + landed[ch * height : (ch + 1) * height, lanes]
            )
    for tile in range(4 * channels):
        block = v_ref[tile, LEAD - 8 : LEAD]
        index = lax.broadcasted_iota(jnp.int32, block.shape, 0)
        near, far = v_ref[tile, LEAD + 1 : LEAD + 2], v_ref[tile, LEAD + 2 : LEAD + 3]
        v_ref[tile, LEAD - 8 : LEAD] = jnp.where(first, jnp.where(index == 7, near, jnp.where(index == 6, far, block)), block)
        block = v_ref[tile, LEAD + height : LEAD + height + 8]
        near = v_ref[tile, LEAD + height - 2 : LEAD + height - 1]
        v_ref[tile, LEAD + height : LEAD + height + 8] = jnp.where(last & (index == 0), near, block)

    up_ref[...] = jnp.zeros_like(up_ref)
    down_ref[...] = jnp.zeros_like(down_ref)
    lane = lax.broadcasted_iota(jnp.int32, (1, 128), 1) + 384
    tiles_of = ((0, 1, 2, 3), (2, 3), (3,), (3,), (3,))
    outs = (t1_ref, t2_ref, t3_ref, t4_ref, t5_ref)
    for k in range(LEVELS):
        n = height >> (k + 1)
        count = rows_of(n)
        source = chain[k]
        before = tiles_of[k - 1] if k else (0, 1, 2, 3)
        mine = (lane == LOW_LANE[k]) | (lane == HIGH_LANE[k])
        if k >= 2:
            mine = mine | (lane >= OWN_LANE[k]) & (lane < OWN_LANE[k] + (64 >> (k - 2)))
        for ch in range(channels):
            for at, t in enumerate(tiles_of[k]):
                tile = ch * len(before) + before.index(t)
                s = [source[tile, pl.ds(6 + i, count, stride=2), :] for i in range(5)]
                r = (s[0] + s[4]) * 0.0625 + (s[1] + s[3]) * 0.25 + s[2] * 0.375
                index = lax.broadcasted_iota(jnp.int32, r.shape, 0)
                r = jnp.where(first & (index == 7), r[9:10], jnp.where(first & (index == 6), r[10:11], r))
                if k < LEVELS - 1 and TILE_LEVELS[t] > k + 1:
                    onward = jnp.where(last & (index == 8 + n), r[6 + n : 7 + n], r)
                    chain[k + 1][ch * len(tiles_of[k]) + at, LEAD - 8 : LEAD - 8 + count] = onward
                if t in TILES[k]:
                    border = jnp.where(last & (index == 8 + n), r[7 + n : 8 + n], r)
                    outs[k][ch * len(TILES[k]) + TILES[k].index(t)] = border
                    going_up, going_down = r[7:9], r[7 + n : 10 + n]
                    if t == 3:
                        going_up = jnp.where(mine, going_up, 0.0) + (up_ref[ch, 9:11] if k else 0.0)
                        going_down = jnp.where(mine, going_down, 0.0) + (down_ref[ch, 9:12] if k else 0.0)
                    up_ref[ch, 3 * t : 3 * t + 2] = going_up
                    down_ref[ch, 3 * t : 3 * t + 3] = going_down


def detail_kernel(
    x_ref, t1_ref, t2_ref, t3_ref, t4_ref, t5_ref, from_up_ref, from_down_ref, e0, e1, e2, e3, e4,
    d0_hbm, d1_hbm, d2_hbm, d3_hbm, d4_hbm, coarsest_hbm,
    o0, o1, o2, o3, o4, n3, n4, n5, s1, s2, s3, s4, s5, y1, y2, y3, y4, y5, sems,
):
    channels, height = x_ref.shape[0], x_ref.shape[1]
    row = lax.axis_index("rows")
    first, last = row == 0, row == lax.axis_size("rows") - 1
    levels, fines = (s1, s2, s3, s4, s5), (o0, o1, o2, o3, o4)
    hbm = (d0_hbm, d1_hbm, d2_hbm, d3_hbm, d4_hbm)
    for ch in range(channels):
        from_up, from_down = jnp.where(first, 0.0, from_up_ref[ch]), jnp.where(last, 0.0, from_down_ref[ch])
        for k, (t_ref, s_ref) in enumerate(zip((t1_ref, t2_ref, t3_ref, t4_ref, t5_ref), levels)):
            n = height >> (k + 1)
            for at, t in enumerate(TILES[k]):
                tile = ch * len(TILES[k]) + at
                s_ref[tile] = t_ref[tile]
                s_ref[tile, 7:10] = s_ref[tile, 7:10] + from_up[3 * t : 3 * t + 3]
                s_ref[tile, 7 + n : 9 + n] = s_ref[tile, 7 + n : 9 + n] + from_down[3 * t : 3 * t + 2]
    copies = []

    def out(source, target, *at):
        copies.append(pltpu.make_async_copy(source, target, sems.at[at]))
        copies[-1].start()

    for k in range(LEVELS):
        n, count, tiles = height >> (k + 1), levels[k].shape[1], len(TILES[k])
        cells = jnp.concatenate(
            [levels[k][...].reshape(channels, tiles, count, 128)[:, at].reshape(channels * count, 128) for at in range(tiles)],
            axis=1,
        )
        y_ref = (y1, y2, y3, y4, y5)[k]
        y = times(cells, (e0, e1, e2, e3, e4)[k][...])
        y_ref[...] = y.reshape(channels, count, y.shape[1])
        wide = y.shape[1] // 128
        for ch in range(channels):
            for at in range(wide):
                lanes = slice(128 * at, 128 * (at + 1))
                fine = fines[k].at[ch * wide + at]
                if k == 0:
                    fine[...] = x_ref[ch, :, lanes]
                else:
                    fine[...] = levels[k - 1][ch * len(TILES[k - 1]) + at, 8 : 8 + 2 * n]
                before, center, after = (y_ref[ch, i : i + n, lanes] for i in (7, 8, 9))
                fine[pl.ds(0, n, stride=2), :] = fine[pl.ds(0, n, stride=2), :] - (before + 6.0 * center + after) * 0.125
                fine[pl.ds(1, n, stride=2), :] = fine[pl.ds(1, n, stride=2), :] - (center + after) * 0.5
                if k < 3:
                    out(fine, hbm[k].at[ch, :, pl.ds(128 * at, 128)], k, ch, at)
                elif k == 3:
                    n3[ch] = fine[:, :64]
                    out(n3.at[ch], d3_hbm.at[ch], k, ch, 0)
                else:
                    n4[ch] = fine[:, 64:96]
                    out(n4.at[ch], d4_hbm.at[ch], k, ch, 0)
                    n5[ch] = levels[k][ch, 8 : 8 + n, 96:112]
                    out(n5.at[ch], coarsest_hbm.at[ch], k, ch, 1)
    for copy in copies:
        copy.wait()


VMEM = pl.BlockSpec(memory_space=pltpu.VMEM)
HBM = pl.BlockSpec(memory_space=pltpu.HBM)


def call(kernel, outs, flops, args, scratch=(), in_space=VMEM, out_space=VMEM, limit=24 * 2**20):
    bytes_of = lambda a: a.size * a.dtype.itemsize
    outs = [jax.ShapeDtypeStruct(*(s if isinstance(s[0], tuple) else (s, F32))) for s in outs]
    return pl.pallas_call(
        kernel,
        out_shape=outs,
        in_specs=[in_space] * len(args),
        out_specs=[out_space] * len(outs),
        scratch_shapes=list(scratch),
        compiler_params=pltpu.CompilerParams(vmem_limit_bytes=limit),
        cost_estimate=pl.CostEstimate(flops=flops, bytes_accessed=sum(bytes_of(a) for a in args), transcendentals=0),
    )(*args)


def permute(x, axis, to):
    count = lax.axis_size(axis)
    return lax.ppermute(x, axis, [(i, to(i) % count) for i in range(count)])


def body(x):
    channels, height, width = x.shape
    c = {name: jnp.asarray(value) for name, value in constants(width).items()}
    side = (channels, 16, height)
    fixed = [c[name] for name in ("edge", "col_a", "col_b", "land")]
    send_b, send_a, low, high, x_near, col_a, col_b, land = call(
        edge_kernel,
        [side] * 4 + [x.shape] + [(a.shape, BF16) for a in fixed[1:]],
        10**8,
        [pltpu.with_memory_space_constraint(a, pltpu.HBM) for a in (x, *fixed)],
        [pltpu.VMEM(c["edge"].shape, BF16), pltpu.SemaphoreType.DMA((7,))],
        HBM,
    )
    got_b, got_a = permute(send_b, "cols", lambda i: i - 1 + 2 * (i % 2)), permute(send_a, "cols", lambda i: i ^ 1)
    (u,) = call(column_kernel, [(channels, height, 512)], 10**9, (x_near, col_a, col_b))
    ns = [height >> (k + 1) for k in range(LEVELS)]
    tall = lambda tiles, n: pltpu.VMEM((tiles * channels, LEAD + n + TAIL, 128), F32)
    message = (channels, 16, 128)
    *t, down, up = call(
        row_kernel,
        [(channels * len(t), rows_of(n), 128) for n, t in zip(ns, TILES)] + [message] * 2,
        10**8,
        (u, got_b, got_a, low, high, land),
        [tall(4, height), tall(4, ns[0]), tall(2, ns[1]), tall(1, ns[2]), tall(1, ns[3])],
    )
    from_up, from_down = permute(down, "rows", lambda i: i + 1), permute(up, "rows", lambda i: i - 1)
    outs = [(channels, height >> k, width >> k) for k in range(LEVELS + 1)]
    return call(
        detail_kernel,
        outs,
        10**9,
        (x_near, *t, from_up, from_down, *(c[f"expand_{k}"] for k in range(LEVELS))),
        [pltpu.VMEM((channels * max(1, width >> (k + 7)), height >> k, 128), F32) for k in range(LEVELS)]
        + [pltpu.VMEM(s, F32) for s in outs[3:]]
        + [pltpu.VMEM((channels * len(t), rows_of(n), 128), F32) for n, t in zip(ns, TILES)]
        + [pltpu.VMEM((channels, rows_of(n), max(128, width >> k)), F32) for k, n in enumerate(ns)]
        + [pltpu.SemaphoreType.DMA((LEVELS, channels, 4))],
        VMEM,
        HBM,
    )


def solution(mesh):
    placed = P(None, "rows", "cols")
    return jax.shard_map(body, mesh=mesh, in_specs=(placed,), out_specs=(placed,) * 6, check_vma=False)
```

time: 29.4 us -> 19.6 us (0.67)
  the two profiles are of different devices: /device:TPU:117 before, /device:TPU:1 now
where the time goes in v1:
time: 19.6 us; the launch traced here: 19.5 us
  starting transfers between devices  12 us (61%)
  Pallas kernels  5.64 us (29%)
  waiting for transfers between devices  1.13 us (6%)
  between operations  0.74 us (4%)
    ppermute x4, starting transfers between devices, permute(): return lax.ppermute(x, axis, [(i, to(i) % count) for i in range(count)])  12 us
    pallas_call x4, Pallas kernels, call(): pl.pallas_call(kernel, out_shape=outs, in_specs=[in_space] * len(args), o...  5.64 us
    ppermute x4, waiting for transfers between devices, permute(): return lax.ppermute(x, axis, [(i, to(i) % count) for i in range(count)])  1.13 us
  transfers between devices with their start and end apart: 4, of which 1 were waited for; matrix products, arithmetic and copies ran while one was open for 0% of the time, Pallas kernels for 5%

profile of v1, /device:TPU:1, one launch (start us, length us, event | category | flops | bytes accessed | tf_op | source)
XLA Modules:
  0.0 19.5 jit_solution(9123705647655521381)
XLA Ops:
  0.6 1.5 %shard_map.145 = (f32[3,16,128]{2,1,0:T(8,128)S(1)}, f32[3,16,128]{2,1,0:T(8,128)S(1)}, f32[3,16,128]{2,1,0:T(8,128)S(1)}, f32[3,16,128]{2,1,0:T(8,128)S(1)}, f3...) custom-call(f32[3,128,512]{2,1,0:T(8,128)} %x_hbm.1, ...), custom_call_target="tpu_custom_call" | custom-call | flops 100000000 | bytes 1507328 | tf_op jit(solution)/shard_map/pallas_call | solution.py:332
  2.1 2.7 %collective-permute-start = (f32[3,16,128]{2,1,0:T(8,128)S(1)}, f32[3,16,128]{2,1,0:T(8,128)S(1)}, u32[]{:S(2)}, u32[]{:S(2)}) collective-permute-start(f32[3,16,128]{2,1,0:T(8,128)S(1)} %get-tuple-element.24), channel_id=1, source_target_pairs={{0,7},{1,2},{2,1},{3,4},{4,3},{5,6},{6,5},{7,0},{8,15},{9,10},{10,... | collective-permute-start | bytes 73736 | tf_op jit(solution)/shard_map/ppermute | solution.py:345
  4.8 1.1 %collective-permute-start.1 = (f32[3,16,128]{2,1,0:T(8,128)S(1)}, f32[3,16,128]{2,1,0:T(8,128)S(1)}, u32[]{:S(2)}, u32[]{:S(2)}) collective-permute-start(f32[3,16,128]{2,1,0:T(8,128)S(1)} %get-tuple-element.25), channel_id=1, source_target_pairs={{0,1},{1,0},{2,3},{3,2},{4,5},{5,4},{6,7},{7,6},{8,9},{9,8},{10,11... | collective-permute-start | bytes 73736 | tf_op jit(solution)/shard_map/ppermute | solution.py:345
  5.9 1.1 %shard_map.146.u_ref = f32[3,128,512]{2,1,0:T(8,128)S(1)} custom-call(f32[3,128,512]{2,1,0:T(8,128)S(1)} %get-tuple-element.21.x_ref, bf16[512,384]{1,0:T(8,128)(2,1)S(1)} %get-tuple-element.22.a_ref, bf16[512,256]{1,0:T(8,128)(2,1)S(1)} %get-tuple-element.23.b_ref), custom_call_target="tpu_custom_call" | custom-call | flops 1000000000 | bytes 1441792 | tf_op jit(solution)/shard_map/pallas_call | solution.py:332
  7.0 0.0 collective-permute-done.got_b_ref
  7.0 0.0 collective-permute-done.1.got_a_ref
  7.0 0.0 copy-start
  7.0 0.0 copy-start.1
  7.0 0.0 copy-start.2
  7.1 0.0 copy-start.3
  7.1 0.0 copy-start.4
  7.1 0.9 %shard_map.147 = (f32[9,80,128]{2,1,0:T(8,128)S(1)}, f32[6,48,128]{2,1,0:T(8,128)S(1)}, f32[3,32,128]{2,1,0:T(8,128)S(1)}, f32[3,24,128]{2,1,0:T(8,128)S(1)}, f3...) custom-call(f32[3,128,512]{2,1,0:T(8,128)S(1)} %shard_map.146.u_ref, ...), custom_call_target="tpu_custom_call" | custom-call | flops 100000000 | bytes 917504 | tf_op jit(solution)/shard_map/pallas_call | solution.py:332
  7.9 1.7 %collective-permute-start.2 = (f32[3,16,128]{2,1,0:T(8,128)S(1)}, f32[3,16,128]{2,1,0:T(8,128)S(1)}, u32[]{:S(2)}, u32[]{:S(2)}) collective-permute-start(f32[3,16,128]{2,1,0:T(8,128)S(1)} %get-tuple-element.34), channel_id=1, source_target_pairs={{0,8},{8,16},{16,24},{24,32},{32,40},{40,48},{48,56},{56,64},{64,7... | collective-permute-start | bytes 73736 | tf_op jit(solution)/shard_map/ppermute | solution.py:345
  9.7 6.5 %collective-permute-start.3 = (f32[3,16,128]{2,1,0:T(8,128)S(1)}, f32[3,16,128]{2,1,0:T(8,128)S(1)}, u32[]{:S(2)}, u32[]{:S(2)}) collective-permute-start(f32[3,16,128]{2,1,0:T(8,128)S(1)} %get-tuple-element.35), channel_id=1, source_target_pairs={{0,248},{8,0},{16,8},{24,16},{32,24},{40,32},{48,40},{56,48},{64,5... | collective-permute-start | bytes 73736 | tf_op jit(solution)/shard_map/ppermute | solution.py:345
  16.1 1.1 %collective-permute-done.2.from_up_ref = f32[3,16,128]{2,1,0:T(8,128)S(1)} collective-permute-done((f32[3,16,128]{2,1,0:T(8,128)S(1)}, f32[3,16,128]{2,1,0:T(8,128)S(1)}, u32[]{:S(2)}, u32[]{:S(2)}) %collective-permute-start.2) | collective-permute-done | bytes 24608 | tf_op jit(solution)/shard_map/ppermute | solution.py:345
  17.3 0.0 collective-permute-done.3.from_down_ref
  17.3 0.0 copy-done
  17.3 0.0 copy-done.1
  17.3 0.0 copy-done.2
  17.3 0.0 copy-done.3
  17.3 0.0 copy-done.4
  17.3 2.2 %shard_map.148 = (f32[3,128,512]{2,1,0:T(8,128)}, f32[3,64,256]{2,1,0:T(8,128)}, f32[3,32,128]{2,1,0:T(8,128)}, f32[3,16,64]{2,1,0:T(8,128)}, f32[3,8,32]{2,1,0:T(8,128)}, /*index=5*/f32[3,4,16]{2,1,0:T(4,128)}) custom-call(f32[3,128,512]{2,1,0:T(8,128)S(1)} %get-tuple-element.21.x_ref, f32[9,80,128]{2,1,0:T(8,128)S(1)} %get-tuple-element.29.t1_ref, ...), custom_call_target="tpu_custom_call" | custom-call | flops 1000000000 | bytes 2097152 | tf_op jit(solution)/shard_map/pallas_call | solution.py:332
Async XLA Ops:
  2.1 4.9 %collective-permute-start = (f32[3,16,128]{2,1,0:T(8,128)S(1)}, f32[3,16,128]{2,1,0:T(8,128)S(1)}, u32[]{:S(2)}, u32[]{:S(2)}) collective-permute-start(f32[3,16,128]{2,1,0:T(8,128)S(1)} %get-tuple-element.24), channel_id=1, source_target_pairs={{0,7},{1,2},{2,1},{3,4},{4,3},{5,6},{6,5},{7,0},{8,15},{9,10},{10,... | collective-permute-start | bytes 73736 | tf_op jit(solution)/shard_map/ppermute | solution.py:345
  4.8 2.2 %collective-permute-start.1 = (f32[3,16,128]{2,1,0:T(8,128)S(1)}, f32[3,16,128]{2,1,0:T(8,128)S(1)}, u32[]{:S(2)}, u32[]{:S(2)}) collective-permute-start(f32[3,16,128]{2,1,0:T(8,128)S(1)} %get-tuple-element.25), channel_id=1, source_target_pairs={{0,1},{1,0},{2,3},{3,2},{4,5},{5,4},{6,7},{7,6},{8,9},{9,8},{10,11... | collective-permute-start | bytes 73736 | tf_op jit(solution)/shard_map/ppermute | solution.py:345
  7.0 10.3 %copy-start = (bf16[384,512]{1,0:T(8,128)(2,1)S(1)}, bf16[384,512]{1,0:T(8,128)(2,1)}, u32[]{:S(2)}) copy-start(bf16[384,512]{1,0:T(8,128)(2,1)} %constant.22.clone.e0) | copy-start | bytes 1179652
  7.0 10.2 %copy-start.1 = (bf16[256,256]{1,0:T(8,128)(2,1)S(1)}, bf16[256,256]{1,0:T(8,128)(2,1)}, u32[]{:S(2)}) copy-start(bf16[256,256]{1,0:T(8,128)(2,1)} %constant.23.clone.e1) | copy-start | bytes 393220
  7.0 10.2 %copy-start.2 = (bf16[128,128]{1,0:T(8,128)(2,1)S(1)}, bf16[128,128]{1,0:T(8,128)(2,1)}, u32[]{:S(2)}) copy-start(bf16[128,128]{1,0:T(8,128)(2,1)} %constant.26.clone.e4) | copy-start | bytes 98308
  7.1 10.2 %copy-start.3 = (bf16[128,128]{1,0:T(8,128)(2,1)S(1)}, bf16[128,128]{1,0:T(8,128)(2,1)}, u32[]{:S(2)}) copy-start(bf16[128,128]{1,0:T(8,128)(2,1)} %constant.25.clone.e3) | copy-start | bytes 98308
  7.1 10.2 %copy-start.4 = (bf16[128,128]{1,0:T(8,128)(2,1)S(1)}, bf16[128,128]{1,0:T(8,128)(2,1)}, u32[]{:S(2)}) copy-start(bf16[128,128]{1,0:T(8,128)(2,1)} %constant.24.clone.e2) | copy-start | bytes 98308
  7.9 9.3 %collective-permute-start.2 = (f32[3,16,128]{2,1,0:T(8,128)S(1)}, f32[3,16,128]{2,1,0:T(8,128)S(1)}, u32[]{:S(2)}, u32[]{:S(2)}) collective-permute-start(f32[3,16,128]{2,1,0:T(8,128)S(1)} %get-tuple-element.34), channel_id=1, source_target_pairs={{0,8},{8,16},{16,24},{24,32},{32,40},{40,48},{48,56},{56,64},{64,7... | collective-permute-start | bytes 73736 | tf_op jit(solution)/shard_map/ppermute | solution.py:345
  9.7 7.6 %collective-permute-start.3 = (f32[3,16,128]{2,1,0:T(8,128)S(1)}, f32[3,16,128]{2,1,0:T(8,128)S(1)}, u32[]{:S(2)}, u32[]{:S(2)}) collective-permute-start(f32[3,16,128]{2,1,0:T(8,128)S(1)} %get-tuple-element.35), channel_id=1, source_target_pairs={{0,248},{8,0},{16,8},{24,16},{32,24},{40,32},{48,40},{56,48},{64,5... | collective-permute-start | bytes 73736 | tf_op jit(solution)/shard_map/ppermute | solution.py:345

commit v2 on v1

--- a/solution.py
+++ b/solution.py
@@ -77,6 +77,7 @@
 OWN_LANE = (0, 256, 384, 448, 480)
 LOW_LANE = tuple(496 + k for k in range(LEVELS))
 HIGH_LANE = tuple(501 + k for k in range(LEVELS))
+COPY_LANE = (506, 507)
 TILES = ((0, 1, 3), (2, 3), (3,), (3,), (3,))
 TILE_LEVELS = (1, 1, 2, 5)
 LEAD = 24
@@ -104,6 +105,8 @@
         m = part.shape[0] - 2
         own[:, OWN_LANE[k] : OWN_LANE[k] + m] = part[1:-1].T
         own[:, LOW_LANE[k]], own[:, HIGH_LANE[k]] = part[0], part[-1]
+        if k == 0:
+            own[:, COPY_LANE[0]], own[:, COPY_LANE[1]] = part[m // 2], part[m // 2 + 1]
     c["col_a"] = exact(own[:, :384], 1)[0]
     c["col_b"] = np.concatenate(exact(own[:, 384:], 2), axis=1)
     land = np.zeros((32, 512))
@@ -114,6 +117,7 @@
         for q, at in enumerate((OWN_LANE[k] + m - 1, HIGH_LANE[k])):
             land[16 + 2 * k + q, at] = 1
     c["land"] = exact(land, 1)[0]
+    third = np.zeros((128, 384))
     for k in range(LEVELS):
         m = width >> (k + 1)
         e = expand_matrix(m).T
@@ -121,15 +125,15 @@
         lanes[OWN_LANE[k] : OWN_LANE[k] + m] = e[1:-1]
         lanes[LOW_LANE[k]], lanes[HIGH_LANE[k]] = e[0], e[-1]
         if k == 0:
-            lanes = np.concatenate([lanes[:256], lanes[384:]])
+            halves = lanes[:, :m].copy(), lanes[:, m:].copy()
+            halves[0][COPY_LANE[1]], halves[1][COPY_LANE[0]] = halves[0][128], halves[1][127]
+            c["expand_0"] = np.concatenate([exact(np.concatenate([halves[i][128 * i : 128 * i + 128], halves[i][384:]]), 1)[0] for i in (0, 1)], axis=1)
+        elif k == 1:
+            c["expand_1"] = exact(lanes[256:], 1)[0]
         else:
-            lanes = lanes[256:] if k == 1 else lanes[384:]
-        if k >= 3:
-            at = OWN_LANE[k - 1] - 384
-            wide = np.zeros((128, 128))
-            wide[:, at : at + 2 * m] = lanes
-            lanes = wide
-        c[f"expand_{k}"] = exact(lanes, 1)[0]
+            at = 128 * (k - 2) + (OWN_LANE[k - 1] - 384 if k > 2 else 0)
+            third[:, at : at + 2 * m] = lanes[384:]
+    c["expand_2"] = exact(third, 1)[0]
     return c
 
 
@@ -152,8 +156,8 @@
     edge_ref, sems,
 ):
     channels, height, width = x_hbm.shape
-    lanes = [pl.ds(0, 128), pl.ds(width - 128, 128), pl.ds(128, width - 256)]
-    pairs = [(edge_hbm, edge_ref)] + [(x_hbm.at[:, :, at], x_ref.at[:, :, at]) for at in lanes]
+    tiles = [0, width // 128 - 1, *range(1, width // 128 - 1)]
+    pairs = [(edge_hbm, edge_ref)] + [(x_hbm.at[:, :, pl.ds(128 * t, 128)], x_ref.at[:, t]) for t in tiles]
     pairs += [(a_hbm, a_ref), (b_hbm, b_ref), (land_hbm, land_ref)]
     copies = [pltpu.make_async_copy(source, target, sems.at[i]) for i, (source, target) in enumerate(pairs)]
     for copy in copies:
@@ -165,7 +169,7 @@
     for side in range(2):
         out = sum(
             lax.dot_general(edge_ref[side], part, (((1,), (1,)), ((), ())), preferred_element_type=F32)
-            for part in split(x_ref[:, :, lanes[side].start : lanes[side].start + 128].reshape(channels * height, 128))
+            for part in split(x_ref[:, tiles[side]].reshape(channels * height, 128))
         )
         sides.append(out[:32] + out[32:])
     left, right = sides
@@ -179,8 +183,8 @@
 
 
 def column_kernel(x_ref, a_ref, b_ref, u_ref):
-    channels, height, width = x_ref.shape
-    x = x_ref[...].reshape(channels * height, width)
+    channels, tiles, height, _ = x_ref.shape
+    x = jnp.concatenate([x_ref[:, t].reshape(channels * height, 128) for t in range(tiles)], axis=1)
     u_ref[:, :, :384] = times(x, a_ref[...]).reshape(channels, height, 384)
     last = times(x, b_ref[...])
     u_ref[:, :, 384:] = (last[:, :128] + last[:, 128:]).reshape(channels, height, 128)
@@ -239,6 +243,8 @@
         source = chain[k]
         before = tiles_of[k - 1] if k else (0, 1, 2, 3)
         mine = (lane == LOW_LANE[k]) | (lane == HIGH_LANE[k])
+        if k == 0:
+            mine = mine | (lane == COPY_LANE[0]) | (lane == COPY_LANE[1])
         if k >= 2:
             mine = mine | (lane >= OWN_LANE[k]) & (lane < OWN_LANE[k] + (64 >> (k - 2)))
         for ch in range(channels):
@@ -256,68 +262,105 @@
                     outs[k][ch * len(TILES[k]) + TILES[k].index(t)] = border
                     going_up, going_down = r[7:9], r[7 + n : 10 + n]
                     if t == 3:
-                        going_up = jnp.where(mine, going_up, 0.0) + (up_ref[ch, 9:11] if k else 0.0)
-                        going_down = jnp.where(mine, going_down, 0.0) + (down_ref[ch, 9:12] if k else 0.0)
-                    up_ref[ch, 3 * t : 3 * t + 2] = going_up
-                    down_ref[ch, 3 * t : 3 * t + 3] = going_down
-
-
-def detail_kernel(
-    x_ref, t1_ref, t2_ref, t3_ref, t4_ref, t5_ref, from_up_ref, from_down_ref, e0, e1, e2, e3, e4,
+                        going_up = jnp.where(mine, going_up, 0.0) + (up_ref[ch, 12:14] if k else 0.0)
+                        going_down = jnp.where(mine, going_down, 0.0) + (down_ref[ch, 12:15] if k else 0.0)
+                    up_ref[ch, 4 * t : 4 * t + 2] = going_up
+                    down_ref[ch, 4 * t : 4 * t + 3] = going_down
+
+
+def own_kernel(x_ref, t1_ref, t2_ref, t3_ref, t4_ref, t5_ref, e0, e1, e2, g0, g1, g2, g3, g4, y1, y2, y3, y4, y5):
+    channels, wide, height, _ = x_ref.shape
+    levels, owns, ys = (t1_ref, t2_ref, t3_ref, t4_ref, t5_ref), (g0, g1, g2, g3, g4), (y1, y2, y3, y4, y5)
+    for k in range(LEVELS):
+        n, count, tiles = height >> (k + 1), levels[k].shape[1], len(TILES[k])
+        cells = levels[k][...].reshape(channels, tiles, count, 128)
+        cells = [cells[:, at].reshape(channels * count, 128) for at in range(tiles)]
+        if k == 0:
+            for half in range(2):
+                y = times(jnp.concatenate([cells[half], cells[2]], axis=1), e0[:, 256 * half : 256 * half + 256])
+                y1[:, :, 256 * half : 256 * half + 256] = y.reshape(channels, count, 256)
+        elif k == 1:
+            y2[...] = times(jnp.concatenate(cells, axis=1), e1[...]).reshape(y2.shape)
+        else:
+            ys[k][...] = times(cells[0], e2[:, 128 * (k - 2) : 128 * (k - 1)]).reshape(ys[k].shape)
+        across = owns[k].shape[0] // channels
+        for ch in range(channels):
+            for at in range(across):
+                lanes = slice(128 * at, 128 * (at + 1))
+                before, center, after = (ys[k][ch, i : i + n, lanes] for i in (7, 8, 9))
+                for phase, part in ((0, (before + 6.0 * center + after) * 0.125), (1, (center + after) * 0.5)):
+                    if k == 0:
+                        fine = x_ref[ch, at, pl.ds(phase, n, stride=2), :]
+                    else:
+                        fine = levels[k - 1][ch * len(TILES[k - 1]) + at, pl.ds(8 + phase, n, stride=2), :]
+                    owns[k][ch * across + at, pl.ds(phase, n, stride=2), :] = fine - part
+
+
+def end_kernel(
+    g0, g1, g2, g3, g4, t5_ref, from_up_ref, from_down_ref, e0, e1, e2,
     d0_hbm, d1_hbm, d2_hbm, d3_hbm, d4_hbm, coarsest_hbm,
-    o0, o1, o2, o3, o4, n3, n4, n5, s1, s2, s3, s4, s5, y1, y2, y3, y4, y5, sems,
+    top0, low0, top1, low1, top2, low2, n3, n4, n5, sems,
 ):
-    channels, height = x_ref.shape[0], x_ref.shape[1]
+    channels = from_up_ref.shape[0]
     row = lax.axis_index("rows")
     first, last = row == 0, row == lax.axis_size("rows") - 1
-    levels, fines = (s1, s2, s3, s4, s5), (o0, o1, o2, o3, o4)
-    hbm = (d0_hbm, d1_hbm, d2_hbm, d3_hbm, d4_hbm)
+    copies = []
+
+    def out(source, target):
+        copies.append(pltpu.make_async_copy(source, target, sems.at[len(copies)]))
+        copies[-1].start()
+
+    for own, hbm in ((g0, d0_hbm), (g1, d1_hbm), (g2, d2_hbm)):
+        across, inner = own.shape[0] // channels, own.shape[1] - 16
+        for tile in range(own.shape[0]):
+            out(own.at[tile, pl.ds(8, inner)], hbm.at[tile // across, pl.ds(8, inner), pl.ds(128 * (tile % across), 128)])
+    r = lax.broadcasted_iota(jnp.int32, (8, 128), 0)
+
+    def weights(*rows):
+        out = jnp.zeros((8, 128), F32)
+        for at, value in rows:
+            out = jnp.where(r == at, value, out)
+        return out
+
+    to_top = (weights((0, 0.125)), weights((0, 0.75), (1, 0.5), (2, 0.125)), weights((0, 0.125), (1, 0.5), (2, 0.75), (3, 0.5), (4, 0.125)))
+    to_low = (weights((4, 0.125), (5, 0.5), (6, 0.75), (7, 0.5)), weights((6, 0.125), (7, 0.5)))
+    coarse, fine = [[] for _ in range(4)], []
     for ch in range(channels):
-        from_up, from_down = jnp.where(first, 0.0, from_up_ref[ch]), jnp.where(last, 0.0, from_down_ref[ch])
-        for k, (t_ref, s_ref) in enumerate(zip((t1_ref, t2_ref, t3_ref, t4_ref, t5_ref), levels)):
-            n = height >> (k + 1)
-            for at, t in enumerate(TILES[k]):
-                tile = ch * len(TILES[k]) + at
-                s_ref[tile] = t_ref[tile]
-                s_ref[tile, 7:10] = s_ref[tile, 7:10] + from_up[3 * t : 3 * t + 3]
-                s_ref[tile, 7 + n : 9 + n] = s_ref[tile, 7 + n : 9 + n] + from_down[3 * t : 3 * t + 2]
-    copies = []
-
-    def out(source, target, *at):
-        copies.append(pltpu.make_async_copy(source, target, sems.at[at]))
-        copies[-1].start()
-
-    for k in range(LEVELS):
-        n, count, tiles = height >> (k + 1), levels[k].shape[1], len(TILES[k])
-        cells = jnp.concatenate(
-            [levels[k][...].reshape(channels, tiles, count, 128)[:, at].reshape(channels * count, 128) for at in range(tiles)],
-            axis=1,
-        )
-        y_ref = (y1, y2, y3, y4, y5)[k]
-        y = times(cells, (e0, e1, e2, e3, e4)[k][...])
-        y_ref[...] = y.reshape(channels, count, y.shape[1])
-        wide = y.shape[1] // 128
-        for ch in range(channels):
-            for at in range(wide):
-                lanes = slice(128 * at, 128 * (at + 1))
-                fine = fines[k].at[ch * wide + at]
-                if k == 0:
-                    fine[...] = x_ref[ch, :, lanes]
-                else:
-                    fine[...] = levels[k - 1][ch * len(TILES[k - 1]) + at, 8 : 8 + 2 * n]
-                before, center, after = (y_ref[ch, i : i + n, lanes] for i in (7, 8, 9))
-                fine[pl.ds(0, n, stride=2), :] = fine[pl.ds(0, n, stride=2), :] - (before + 6.0 * center + after) * 0.125
-                fine[pl.ds(1, n, stride=2), :] = fine[pl.ds(1, n, stride=2), :] - (center + after) * 0.5
-                if k < 3:
-                    out(fine, hbm[k].at[ch, :, pl.ds(128 * at, 128)], k, ch, at)
-                elif k == 3:
-                    n3[ch] = fine[:, :64]
-                    out(n3.at[ch], d3_hbm.at[ch], k, ch, 0)
-                else:
-                    n4[ch] = fine[:, 64:96]
-                    out(n4.at[ch], d4_hbm.at[ch], k, ch, 0)
-                    n5[ch] = levels[k][ch, 8 : 8 + n, 96:112]
-                    out(n5.at[ch], coarsest_hbm.at[ch], k, ch, 1)
+        fine.append([])
+        for t in range(4):
+            up = jnp.where(first, 0.0, from_up_ref[ch, 4 * t : 4 * t + 3])
+            down = jnp.where(last, 0.0, from_down_ref[ch, 4 * t : 4 * t + 2])
+            coarse[t].append(sum(w * up[i : i + 1] for i, w in enumerate(to_top)))
+            coarse[t].append(sum(w * down[i : i + 1] for i, w in enumerate(to_low)))
+            fine[ch].append(
+                (jnp.where(r == 0, up[1:2], jnp.where(r == 1, up[2:3], 0.0)), jnp.where(r == 7, down[:1], 0.0), down[:1])
+            )
+    coarse = [jnp.concatenate(tiles, axis=0) for tiles in coarse]
+    e = [times(jnp.concatenate([coarse[half], coarse[3]], axis=1), e0[:, 256 * half : 256 * half + 256]) for half in range(2)]
+    e.append(times(jnp.concatenate([coarse[2], coarse[3]], axis=1), e1[...]))
+    e.append(times(coarse[3], e2[...]))
+    for ch in range(channels):
+        top, low = slice(16 * ch, 16 * ch + 8), slice(16 * ch + 8, 16 * ch + 16)
+        for t in range(4):
+            lanes, part = slice(128 * t, 128 * (t + 1)), e[t // 2][:, 128 * (t % 2) : 128 * (t % 2) + 128]
+            top0[ch, :, lanes] = g0[4 * ch + t, :8] - part[top]
+            low0[ch, :, lanes] = g0[4 * ch + t, -8:] - part[low]
+        for t in range(2):
+            lanes = slice(128 * t, 128 * (t + 1))
+            top1[ch, :, lanes] = g1[2 * ch + t, :8] + fine[ch][t][0] - e[2][top, lanes]
+            low1[ch, :, lanes] = g1[2 * ch + t, -8:] + fine[ch][t][1] - e[2][low, lanes]
+        top2[ch] = g2[ch, :8] + fine[ch][2][0] - e[3][top, :128]
+        low2[ch] = g2[ch, -8:] + fine[ch][2][1] - e[3][low, :128]
+        n3[ch, :8] = (g3[ch, :8] + fine[ch][3][0] - e[3][top, 128:256])[:, :64]
+        n3[ch, 8:] = (g3[ch, 8:] + fine[ch][3][1] - e[3][low, 128:256])[:, :64]
+        n4[ch] = (g4[ch] + fine[ch][3][0] + fine[ch][3][1] - e[3][top, 256:] - e[3][low, 256:])[:, 64:96]
+        n5[ch] = (t5_ref[ch, 8:16] + fine[ch][3][0] + jnp.where(r == 3, fine[ch][3][2], 0.0))[:4, 96:112]
+    for top, low, hbm in ((top0, low0, d0_hbm), (top1, low1, d1_hbm), (top2, low2, d2_hbm)):
+        out(top, hbm.at[:, pl.ds(0, 8)])
+        out(low, hbm.at[:, pl.ds(hbm.shape[1] - 8, 8)])
+    out(n3, d3_hbm)
+    out(n4, d4_hbm)
+    out(n5, coarsest_hbm)
     for copy in copies:
         copy.wait()
 
@@ -352,10 +395,10 @@
     fixed = [c[name] for name in ("edge", "col_a", "col_b", "land")]
     send_b, send_a, low, high, x_near, col_a, col_b, land = call(
         edge_kernel,
-        [side] * 4 + [x.shape] + [(a.shape, BF16) for a in fixed[1:]],
+        [side] * 4 + [(channels, width // 128, height, 128)] + [(a.shape, BF16) for a in fixed[1:]],
         10**8,
         [pltpu.with_memory_space_constraint(a, pltpu.HBM) for a in (x, *fixed)],
-        [pltpu.VMEM(c["edge"].shape, BF16), pltpu.SemaphoreType.DMA((7,))],
+        [pltpu.VMEM(c["edge"].shape, BF16), pltpu.SemaphoreType.DMA((8,))],
         HBM,
     )
     got_b, got_a = permute(send_b, "cols", lambda i: i - 1 + 2 * (i % 2)), permute(send_a, "cols", lambda i: i ^ 1)
@@ -371,17 +414,23 @@
         [tall(4, height), tall(4, ns[0]), tall(2, ns[1]), tall(1, ns[2]), tall(1, ns[3])],
     )
     from_up, from_down = permute(down, "rows", lambda i: i + 1), permute(up, "rows", lambda i: i - 1)
+    expand = [c[f"expand_{k}"] for k in range(3)]
+    own = call(
+        own_kernel,
+        [(channels * max(1, width >> (k + 7)), height >> k, 128) for k in range(LEVELS)],
+        10**9,
+        (x_near, *t, *expand),
+        [pltpu.VMEM((channels, rows_of(n), max(128, width >> k)), F32) for k, n in enumerate(ns)],
+    )
     outs = [(channels, height >> k, width >> k) for k in range(LEVELS + 1)]
     return call(
-        detail_kernel,
+        end_kernel,
         outs,
-        10**9,
-        (x_near, *t, from_up, from_down, *(c[f"expand_{k}"] for k in range(LEVELS))),
-        [pltpu.VMEM((channels * max(1, width >> (k + 7)), height >> k, 128), F32) for k in range(LEVELS)]
+        10**8,
+        (*own, t[-1], from_up, from_down, *expand),
+        [pltpu.VMEM((channels, 8, s[2]), F32) for s in outs[:3] for _ in range(2)]
         + [pltpu.VMEM(s, F32) for s in outs[3:]]
-        + [pltpu.VMEM((channels * len(t), rows_of(n), 128), F32) for n, t in zip(ns, TILES)]
-        + [pltpu.VMEM((channels, rows_of(n), max(128, width >> k)), F32) for k, n in enumerate(ns)]
-        + [pltpu.SemaphoreType.DMA((LEVELS, channels, 4))],
+        + [pltpu.SemaphoreType.DMA((30,))],
         VMEM,
         HBM,
     )

time: 19.6 us -> 18.7 us (0.954)
  waiting for transfers between devices: 1.13 us -> 0.43 us
    ppermute x4, waiting for transfers between devices: 1.13 us -> 0.43 us  [permute(): return lax.ppermute(x, axis, [(i, to(i) % count) for i in range(count)])]
    pallas_call x4 -> x5, Pallas kernels: 5.64 us -> 5.46 us  [call(): pl.pallas_call(kernel, out_shape=outs, in_specs=[in_space] * len(args), o...]
  transfers between devices with their start and end apart: 4 -> 4, of which waited for: 1 -> 1; matrix products, arithmetic and copies ran while one was open for 0% -> 0% of each run, Pallas kernels for 5% -> 10%
where the time goes in v2:
time: 18.7 us; the launch traced here: 18.6 us
  starting transfers between devices  12 us (64%)
  Pallas kernels  5.46 us (29%)
  between operations  0.71 us (4%)
  waiting for transfers between devices  0.43 us (2%)
    ppermute x4, starting transfers between devices, permute(): return lax.ppermute(x, axis, [(i, to(i) % count) for i in range(count)])  12 us
    pallas_call x5, Pallas kernels, call(): pl.pallas_call(kernel, out_shape=outs, in_specs=[in_space] * len(args), o...  5.46 us
    ppermute x4, waiting for transfers between devices, permute(): return lax.ppermute(x, axis, [(i, to(i) % count) for i in range(count)])  0.43 us
  transfers between devices with their start and end apart: 4, of which 1 were waited for; matrix products, arithmetic and copies ran while one was open for 0% of the time, Pallas kernels for 10%

profile of v2, /device:TPU:1, one launch (start us, length us, event | category | flops | bytes accessed | tf_op | source)
XLA Modules:
  0.0 18.6 jit_solution(5344785503302553890)
XLA Ops:
  0.6 1.5 %shard_map.127 = (f32[3,16,128]{2,1,0:T(8,128)S(1)}, f32[3,16,128]{2,1,0:T(8,128)S(1)}, f32[3,16,128]{2,1,0:T(8,128)S(1)}, f32[3,16,128]{2,1,0:T(8,128)S(1)}, f3...) custom-call(f32[3,128,512]{2,1,0:T(8,128)} %x_hbm.1, ...), custom_call_target="tpu_custom_call" | custom-call | flops 100000000 | bytes 1507328 | tf_op jit(solution)/shard_map/pallas_call | solution.py:375
  2.2 2.7 %collective-permute-start = (f32[3,16,128]{2,1,0:T(8,128)S(1)}, f32[3,16,128]{2,1,0:T(8,128)S(1)}, u32[]{:S(2)}, u32[]{:S(2)}) collective-permute-start(f32[3,16,128]{2,1,0:T(8,128)S(1)} %get-tuple-element.29), channel_id=1, source_target_pairs={{0,7},{1,2},{2,1},{3,4},{4,3},{5,6},{6,5},{7,0},{8,15},{9,10},{10,... | collective-permute-start | bytes 73736 | tf_op jit(solution)/shard_map/ppermute | solution.py:388
  4.8 1.1 %collective-permute-start.1 = (f32[3,16,128]{2,1,0:T(8,128)S(1)}, f32[3,16,128]{2,1,0:T(8,128)S(1)}, u32[]{:S(2)}, u32[]{:S(2)}) collective-permute-start(f32[3,16,128]{2,1,0:T(8,128)S(1)} %get-tuple-element.30), channel_id=1, source_target_pairs={{0,1},{1,0},{2,3},{3,2},{4,5},{5,4},{6,7},{7,6},{8,9},{9,8},{10,11... | collective-permute-start | bytes 73736 | tf_op jit(solution)/shard_map/ppermute | solution.py:388
  5.9 1.1 %shard_map.128.u_ref = f32[3,128,512]{2,1,0:T(8,128)S(1)} custom-call(f32[3,4,128,128]{3,2,1,0:T(8,128)S(1)} %get-tuple-element.26.x_ref, bf16[512,384]{1,0:T(8,128)(2,1)S(1)} %get-tuple-element.27.a_ref, bf16[512,256]{1,0:T(8,128)(2,1)S(1)} %get-tuple-element.28.b_ref), custom_call_target="tpu_custom_call" | custom-call | flops 1000000000 | bytes 1441792 | tf_op jit(solution)/shard_map/pallas_call | solution.py:375
  7.0 0.0 collective-permute-done.got_b_ref
  7.0 0.0 collective-permute-done.1.got_a_ref
  7.1 0.0 copy-start
  7.1 0.0 copy-start.1
  7.1 0.0 copy-start.2
  7.1 0.8 %shard_map.129 = (f32[9,80,128]{2,1,0:T(8,128)S(1)}, f32[6,48,128]{2,1,0:T(8,128)S(1)}, f32[3,32,128]{2,1,0:T(8,128)S(1)}, f32[3,24,128]{2,1,0:T(8,128)S(1)}, f3...) custom-call(f32[3,128,512]{2,1,0:T(8,128)S(1)} %shard_map.128.u_ref, ...), custom_call_target="tpu_custom_call" | custom-call | flops 100000000 | bytes 917504 | tf_op jit(solution)/shard_map/pallas_call | solution.py:375
  8.0 1.7 %collective-permute-start.2 = (f32[3,16,128]{2,1,0:T(8,128)S(1)}, f32[3,16,128]{2,1,0:T(8,128)S(1)}, u32[]{:S(2)}, u32[]{:S(2)}) collective-permute-start(f32[3,16,128]{2,1,0:T(8,128)S(1)} %get-tuple-element.44), channel_id=1, source_target_pairs={{0,8},{8,16},{16,24},{24,32},{32,40},{40,48},{48,56},{56,64},{64,7... | collective-permute-start | bytes 73736 | tf_op jit(solution)/shard_map/ppermute | solution.py:388
  9.7 6.5 %collective-permute-start.3 = (f32[3,16,128]{2,1,0:T(8,128)S(1)}, f32[3,16,128]{2,1,0:T(8,128)S(1)}, u32[]{:S(2)}, u32[]{:S(2)}) collective-permute-start(f32[3,16,128]{2,1,0:T(8,128)S(1)} %get-tuple-element.45), channel_id=1, source_target_pairs={{0,248},{8,0},{16,8},{24,16},{32,24},{40,32},{48,40},{56,48},{64,5... | collective-permute-start | bytes 73736 | tf_op jit(solution)/shard_map/ppermute | solution.py:388
  16.1 0.0 copy-done
  16.2 0.0 copy-done.1
  16.2 0.0 copy-done.2
  16.2 0.7 %shard_map.130 = (f32[12,128,128]{2,1,0:T(8,128)S(1)}, f32[6,64,128]{2,1,0:T(8,128)S(1)}, f32[3,32,128]{2,1,0:T(8,128)S(1)}, f32[3,16,128]{2,1,0:T(8,128)S(1)}, f32[3,8,128]{2,1,0:T(8,128)S(1)}) custom-call(f32[3,4,128,128]{3,2,1,0:T(8,128)S(1)} %get-tuple-element.26.x_ref, f32[9,80,128]{2,1,0:T(8,128)S(1)} %get-tuple-element.34.t1_ref, ...), custom_call_target="tpu_custom_call" | custom-call | flops 1000000000 | bytes 1916928 | tf_op jit(solution)/shard_map/pallas_call | solution.py:375
  16.9 0.4 %collective-permute-done.2.from_up_ref = f32[3,16,128]{2,1,0:T(8,128)S(1)} collective-permute-done((f32[3,16,128]{2,1,0:T(8,128)S(1)}, f32[3,16,128]{2,1,0:T(8,128)S(1)}, u32[]{:S(2)}, u32[]{:S(2)}) %collective-permute-start.2) | collective-permute-done | bytes 24608 | tf_op jit(solution)/shard_map/ppermute | solution.py:388
  17.3 0.0 collective-permute-done.3.from_down_ref
  17.3 1.3 %shard_map.131 = (f32[3,128,512]{2,1,0:T(8,128)}, f32[3,64,256]{2,1,0:T(8,128)}, f32[3,32,128]{2,1,0:T(8,128)}, f32[3,16,64]{2,1,0:T(8,128)}, f32[3,8,32]{2,1,0:T(8,128)}, /*index=5*/f32[3,4,16]{2,1,0:T(4,128)}) custom-call(f32[12,128,128]{2,1,0:T(8,128)S(1)} %get-tuple-element.39.g0, f32[6,64,128]{2,1,0:T(8,128)S(1)} %get-tuple-element.40.g1, ...), custom_call_target="tpu_custom_call" | custom-call | flops 100000000 | bytes 1646592 | tf_op jit(solution)/shard_map/pallas_call | solution.py:375
Async XLA Ops:
  2.2 4.9 %collective-permute-start = (f32[3,16,128]{2,1,0:T(8,128)S(1)}, f32[3,16,128]{2,1,0:T(8,128)S(1)}, u32[]{:S(2)}, u32[]{:S(2)}) collective-permute-start(f32[3,16,128]{2,1,0:T(8,128)S(1)} %get-tuple-element.29), channel_id=1, source_target_pairs={{0,7},{1,2},{2,1},{3,4},{4,3},{5,6},{6,5},{7,0},{8,15},{9,10},{10,... | collective-permute-start | bytes 73736 | tf_op jit(solution)/shard_map/ppermute | solution.py:388
  4.8 2.2 %collective-permute-start.1 = (f32[3,16,128]{2,1,0:T(8,128)S(1)}, f32[3,16,128]{2,1,0:T(8,128)S(1)}, u32[]{:S(2)}, u32[]{:S(2)}) collective-permute-start(f32[3,16,128]{2,1,0:T(8,128)S(1)} %get-tuple-element.30), channel_id=1, source_target_pairs={{0,1},{1,0},{2,3},{3,2},{4,5},{5,4},{6,7},{7,6},{8,9},{9,8},{10,11... | collective-permute-start | bytes 73736 | tf_op jit(solution)/shard_map/ppermute | solution.py:388
  7.1 9.1 %copy-start = (bf16[256,512]{1,0:T(8,128)(2,1)S(1)}, bf16[256,512]{1,0:T(8,128)(2,1)}, u32[]{:S(2)}) copy-start(bf16[256,512]{1,0:T(8,128)(2,1)} %constant.18.clone.e0) | copy-start | bytes 786436
  7.1 9.1 %copy-start.1 = (bf16[256,256]{1,0:T(8,128)(2,1)S(1)}, bf16[256,256]{1,0:T(8,128)(2,1)}, u32[]{:S(2)}) copy-start(bf16[256,256]{1,0:T(8,128)(2,1)} %constant.19.clone.e1) | copy-start | bytes 393220
  7.1 9.1 %copy-start.2 = (bf16[128,384]{1,0:T(8,128)(2,1)S(1)}, bf16[128,384]{1,0:T(8,128)(2,1)}, u32[]{:S(2)}) copy-start(bf16[128,384]{1,0:T(8,128)(2,1)} %constant.20.clone.e2) | copy-start | bytes 294916
  8.0 9.3 %collective-permute-start.2 = (f32[3,16,128]{2,1,0:T(8,128)S(1)}, f32[3,16,128]{2,1,0:T(8,128)S(1)}, u32[]{:S(2)}, u32[]{:S(2)}) collective-permute-start(f32[3,16,128]{2,1,0:T(8,128)S(1)} %get-tuple-element.44), channel_id=1, source_target_pairs={{0,8},{8,16},{16,24},{24,32},{32,40},{40,48},{48,56},{56,64},{64,7... | collective-permute-start | bytes 73736 | tf_op jit(solution)/shard_map/ppermute | solution.py:388
  9.7 7.6 %collective-permute-start.3 = (f32[3,16,128]{2,1,0:T(8,128)S(1)}, f32[3,16,128]{2,1,0:T(8,128)S(1)}, u32[]{:S(2)}, u32[]{:S(2)}) collective-permute-start(f32[3,16,128]{2,1,0:T(8,128)S(1)} %get-tuple-element.45), channel_id=1, source_target_pairs={{0,248},{8,0},{16,8},{24,16},{32,24},{40,32},{48,40},{56,48},{64,5... | collective-permute-start | bytes 73736 | tf_op jit(solution)/shard_map/ppermute | solution.py:388

commit v3 on v2

--- a/solution.py
+++ b/solution.py
@@ -8,6 +8,7 @@
 from jax.experimental import pallas as pl
 from jax.experimental.pallas import tpu as pltpu
 from jax.sharding import PartitionSpec as P
+
 
 LEVELS = 5
 F32 = jnp.float32
@@ -190,20 +191,15 @@
     u_ref[:, :, 384:] = (last[:, :128] + last[:, 128:]).reshape(channels, height, 128)
 
 
-def with_row(rows, at, when, new):
-    index = lax.broadcasted_iota(jnp.int32, rows.shape, 1)
-    return jnp.where((index == at) & when, new, rows)
-
-
 def row_kernel(
     u_ref, got_b_ref, got_a_ref, low_ref, high_ref, land_ref,
-    t1_ref, t2_ref, t3_ref, t4_ref, t5_ref, down_ref, up_ref,
-    v_ref, c1_ref, c2_ref, c3_ref, c4_ref,
+    t1_ref, t2_ref, t3_ref, t4_ref, t5_ref, send_b_ref, send_a_ref,
+    v_ref, c1_ref, c2_ref, c3_ref, c4_ref, up_ref, down_ref,
 ):
     channels, height = u_ref.shape[0], u_ref.shape[1]
     col, row = lax.axis_index("cols"), lax.axis_index("rows")
     col_odd = col % 2 == 1
-    first, last = row == 0, row == lax.axis_size("rows") - 1
+    row_odd, first, last = row % 2 == 1, row == 0, row == lax.axis_size("rows") - 1
     got = []
     for ch in range(channels):
         b, a = got_b_ref[ch], got_a_ref[ch]
@@ -266,10 +262,12 @@
                         going_down = jnp.where(mine, going_down, 0.0) + (down_ref[ch, 12:15] if k else 0.0)
                     up_ref[ch, 4 * t : 4 * t + 2] = going_up
                     down_ref[ch, 4 * t : 4 * t + 3] = going_down
+    send_b_ref[...] = jnp.where(row_odd, down_ref[...], up_ref[...])
+    send_a_ref[...] = jnp.where(row_odd, up_ref[...], down_ref[...])
 
 
 def own_kernel(x_ref, t1_ref, t2_ref, t3_ref, t4_ref, t5_ref, e0, e1, e2, g0, g1, g2, g3, g4, y1, y2, y3, y4, y5):
-    channels, wide, height, _ = x_ref.shape
+    channels, _, height, _ = x_ref.shape
     levels, owns, ys = (t1_ref, t2_ref, t3_ref, t4_ref, t5_ref), (g0, g1, g2, g3, g4), (y1, y2, y3, y4, y5)
     for k in range(LEVELS):
         n, count, tiles = height >> (k + 1), levels[k].shape[1], len(TILES[k])
@@ -296,13 +294,18 @@
                     owns[k][ch * across + at, pl.ds(phase, n, stride=2), :] = fine - part
 
 
+def early(row):
+    return (row % 8 == 2) | ((row % 8 == 0) & (row > 0))
+
+
 def end_kernel(
-    g0, g1, g2, g3, g4, t5_ref, from_up_ref, from_down_ref, e0, e1, e2,
+    g0, g1, g2, g3, g4, t5_ref, got_e_ref, got_b_ref, got_a_ref, e0, e1, e2,
     d0_hbm, d1_hbm, d2_hbm, d3_hbm, d4_hbm, coarsest_hbm,
     top0, low0, top1, low1, top2, low2, n3, n4, n5, sems,
 ):
-    channels = from_up_ref.shape[0]
+    channels = got_b_ref.shape[0]
     row = lax.axis_index("rows")
+    odd = row % 2 == 1
     first, last = row == 0, row == lax.axis_size("rows") - 1
     copies = []
 
@@ -327,9 +330,10 @@
     coarse, fine = [[] for _ in range(4)], []
     for ch in range(channels):
         fine.append([])
+        b, a = got_b_ref[ch], jnp.where(early(row - row % 2), got_e_ref[ch], got_a_ref[ch])
+        from_up, from_down = jnp.where(first, 0.0, jnp.where(odd, a, b)), jnp.where(last, 0.0, jnp.where(odd, b, a))
         for t in range(4):
-            up = jnp.where(first, 0.0, from_up_ref[ch, 4 * t : 4 * t + 3])
-            down = jnp.where(last, 0.0, from_down_ref[ch, 4 * t : 4 * t + 2])
+            up, down = from_up[4 * t : 4 * t + 3], from_down[4 * t : 4 * t + 2]
             coarse[t].append(sum(w * up[i : i + 1] for i, w in enumerate(to_top)))
             coarse[t].append(sum(w * down[i : i + 1] for i, w in enumerate(to_low)))
             fine[ch].append(
@@ -383,9 +387,18 @@
     )(*args)
 
 
-def permute(x, axis, to):
-    count = lax.axis_size(axis)
-    return lax.ppermute(x, axis, [(i, to(i) % count) for i in range(count)])
+def swap(x, mesh_axis, pairs, spare):
+    rows, cols = lax.axis_size("rows"), lax.axis_size("cols")
+    partner = dict(pairs) | {j: i for i, j in pairs}
+    to = []
+    for r in range(rows):
+        for c in range(cols):
+            if mesh_axis == "rows":
+                target = (partner[r], c) if r in partner else spare(r, c)
+            else:
+                target = (r, partner[c]) if c in partner else spare(r, c)
+            to.append(target[0] * cols + target[1])
+    return lax.ppermute(x, ("rows", "cols"), list(enumerate(to)))
 
 
 def body(x):
@@ -401,19 +414,26 @@
         [pltpu.VMEM(c["edge"].shape, BF16), pltpu.SemaphoreType.DMA((8,))],
         HBM,
     )
-    got_b, got_a = permute(send_b, "cols", lambda i: i - 1 + 2 * (i % 2)), permute(send_a, "cols", lambda i: i ^ 1)
+    rows, cols = lax.axis_size("rows"), lax.axis_size("cols")
+    pairs = lambda first, count: [(i, i + 1) for i in range(first, count - 1, 2)]
+    got_b = swap(send_b, "cols", pairs(1, cols), lambda r, c: (r ^ 1, c))
+    got_a = swap(send_a, "cols", pairs(0, cols), None)
     (u,) = call(column_kernel, [(channels, height, 512)], 10**9, (x_near, col_a, col_b))
     ns = [height >> (k + 1) for k in range(LEVELS)]
     tall = lambda tiles, n: pltpu.VMEM((tiles * channels, LEAD + n + TAIL, 128), F32)
     message = (channels, 16, 128)
-    *t, down, up = call(
+    *t, send_b, send_a = call(
         row_kernel,
         [(channels * len(t), rows_of(n), 128) for n, t in zip(ns, TILES)] + [message] * 2,
         10**8,
         (u, got_b, got_a, low, high, land),
-        [tall(4, height), tall(4, ns[0]), tall(2, ns[1]), tall(1, ns[2]), tall(1, ns[3])],
+        [tall(4, height), tall(4, ns[0]), tall(2, ns[1]), tall(1, ns[2]), tall(1, ns[3])]
+        + [pltpu.VMEM(message, F32)] * 2,
     )
-    from_up, from_down = permute(down, "rows", lambda i: i + 1), permute(up, "rows", lambda i: i - 1)
+    beside = lambda r, c: (r, c ^ 1)
+    got_e = swap(send_a, "rows", [p for p in pairs(0, rows) if early(p[0])], beside)
+    got_b = swap(send_b, "rows", pairs(1, rows), beside)
+    got_a = swap(send_a, "rows", [p for p in pairs(0, rows) if not early(p[0])], beside)
     expand = [c[f"expand_{k}"] for k in range(3)]
     own = call(
         own_kernel,
@@ -427,7 +447,7 @@
         end_kernel,
         outs,
         10**8,
-        (*own, t[-1], from_up, from_down, *expand),
+        (*own, t[-1], got_e, got_b, got_a, *expand),
         [pltpu.VMEM((channels, 8, s[2]), F32) for s in outs[:3] for _ in range(2)]
         + [pltpu.VMEM(s, F32) for s in outs[3:]]
         + [pltpu.SemaphoreType.DMA((30,))],

time: 18.7 us -> 17.5 us (0.936)
  the two profiles are of different devices: /device:TPU:1 before, /device:TPU:25 now
where the time goes in v3:
time: 17.5 us; the launch traced here: 17.3 us
  starting transfers between devices  10.3 us (59%)
  Pallas kernels  5.43 us (31%)
  waiting for transfers between devices  0.89 us (5%)
  between operations  0.7 us (4%)
    ppermute x5, starting transfers between devices, swap(): return lax.ppermute(x, ('rows', 'cols'), list(enumerate(to)))  10.3 us
    pallas_call x5, Pallas kernels, call(): pl.pallas_call(kernel, out_shape=outs, in_specs=[in_space] * len(args), o...  5.43 us
    ppermute x5, waiting for transfers between devices, swap(): return lax.ppermute(x, ('rows', 'cols'), list(enumerate(to)))  0.89 us
  transfers between devices with their start and end apart: 5, of which 1 were waited for; matrix products, arithmetic and copies ran while one was open for 0% of the time, Pallas kernels for 10%

profile of v3, /device:TPU:25, one launch (start us, length us, event | category | flops | bytes accessed | tf_op | source)
XLA Modules:
  0.0 17.3 jit_solution(4966042645310323560)
XLA Ops:
  0.6 1.5 %shard_map.127 = (f32[3,16,128]{2,1,0:T(8,128)S(1)}, f32[3,16,128]{2,1,0:T(8,128)S(1)}, f32[3,16,128]{2,1,0:T(8,128)S(1)}, f32[3,16,128]{2,1,0:T(8,128)S(1)}, f3...) custom-call(f32[3,128,512]{2,1,0:T(8,128)} %x_hbm.1, ...), custom_call_target="tpu_custom_call" | custom-call | flops 100000000 | bytes 1507328 | tf_op jit(solution)/shard_map/pallas_call | solution.py:379
  2.2 1.9 %collective-permute-start = (f32[3,16,128]{2,1,0:T(8,128)S(1)}, f32[3,16,128]{2,1,0:T(8,128)S(1)}, u32[]{:S(2)}, u32[]{:S(2)}) collective-permute-start(f32[3,16,128]{2,1,0:T(8,128)S(1)} %get-tuple-element.29), channel_id=1, source_target_pairs={{0,8},{1,2},{2,1},{3,4},{4,3},{5,6},{6,5},{7,15},{8,0},{9,10},{10,... | collective-permute-start | bytes 73736 | tf_op jit(solution)/shard_map/ppermute | solution.py:401
  4.0 0.8 %collective-permute-start.1 = (f32[3,16,128]{2,1,0:T(8,128)S(1)}, f32[3,16,128]{2,1,0:T(8,128)S(1)}, u32[]{:S(2)}, u32[]{:S(2)}) collective-permute-start(f32[3,16,128]{2,1,0:T(8,128)S(1)} %get-tuple-element.30), channel_id=1, source_target_pairs={{0,1},{1,0},{2,3},{3,2},{4,5},{5,4},{6,7},{7,6},{8,9},{9,8},{10,11... | collective-permute-start | bytes 73736 | tf_op jit(solution)/shard_map/ppermute | solution.py:401
  4.8 1.1 %shard_map.128.u_ref = f32[3,128,512]{2,1,0:T(8,128)S(1)} custom-call(f32[3,4,128,128]{3,2,1,0:T(8,128)S(1)} %get-tuple-element.26.x_ref, bf16[512,384]{1,0:T(8,128)(2,1)S(1)} %get-tuple-element.27.a_ref, bf16[512,256]{1,0:T(8,128)(2,1)S(1)} %get-tuple-element.28.b_ref), custom_call_target="tpu_custom_call" | custom-call | flops 1000000000 | bytes 1441792 | tf_op jit(solution)/shard_map/pallas_call | solution.py:379
  5.9 0.0 collective-permute-done.got_b_ref
  5.9 0.0 collective-permute-done.1.got_a_ref
  6.0 0.0 copy-start
  6.0 0.0 copy-start.1
  6.0 0.0 copy-start.2
  6.0 0.9 %shard_map.129 = (f32[9,80,128]{2,1,0:T(8,128)S(1)}, f32[6,48,128]{2,1,0:T(8,128)S(1)}, f32[3,32,128]{2,1,0:T(8,128)S(1)}, f32[3,24,128]{2,1,0:T(8,128)S(1)}, f3...) custom-call(f32[3,128,512]{2,1,0:T(8,128)S(1)} %shard_map.128.u_ref, ...), custom_call_target="tpu_custom_call" | custom-call | flops 100000000 | bytes 917504 | tf_op jit(solution)/shard_map/pallas_call | solution.py:379
  6.9 0.9 %collective-permute-start.4 = (f32[3,16,128]{2,1,0:T(8,128)S(1)}, f32[3,16,128]{2,1,0:T(8,128)S(1)}, u32[]{:S(2)}, u32[]{:S(2)}) collective-permute-start(f32[3,16,128]{2,1,0:T(8,128)S(1)} %get-tuple-element.44), channel_id=1, source_target_pairs={{0,8},{1,9},{2,10},{3,11},{4,12},{5,13},{6,14},{7,15},{8,0},{9,1},... | collective-permute-start | bytes 73736 | tf_op jit(solution)/shard_map/ppermute | solution.py:401
  7.7 1.6 %collective-permute-start.2 = (f32[3,16,128]{2,1,0:T(8,128)S(1)}, f32[3,16,128]{2,1,0:T(8,128)S(1)}, u32[]{:S(2)}, u32[]{:S(2)}) collective-permute-start(f32[3,16,128]{2,1,0:T(8,128)S(1)} %get-tuple-element.44), channel_id=1, source_target_pairs={{0,1},{1,0},{2,3},{3,2},{4,5},{5,4},{6,7},{7,6},{8,9},{9,8},{10,11... | collective-permute-start | bytes 73736 | tf_op jit(solution)/shard_map/ppermute | solution.py:401
  9.3 5.1 %collective-permute-start.3 = (f32[3,16,128]{2,1,0:T(8,128)S(1)}, f32[3,16,128]{2,1,0:T(8,128)S(1)}, u32[]{:S(2)}, u32[]{:S(2)}) collective-permute-start(f32[3,16,128]{2,1,0:T(8,128)S(1)} %get-tuple-element.45), channel_id=1, source_target_pairs={{0,1},{1,0},{2,3},{3,2},{4,5},{5,4},{6,7},{7,6},{8,16},{9,17},{10,... | collective-permute-start | bytes 73736 | tf_op jit(solution)/shard_map/ppermute | solution.py:401
  14.5 0.0 copy-done
  14.5 0.0 copy-done.1
  14.5 0.0 copy-done.2
  14.5 0.7 %shard_map.130 = (f32[12,128,128]{2,1,0:T(8,128)S(1)}, f32[6,64,128]{2,1,0:T(8,128)S(1)}, f32[3,32,128]{2,1,0:T(8,128)S(1)}, f32[3,16,128]{2,1,0:T(8,128)S(1)}, f32[3,8,128]{2,1,0:T(8,128)S(1)}) custom-call(f32[3,4,128,128]{3,2,1,0:T(8,128)S(1)} %get-tuple-element.26.x_ref, f32[9,80,128]{2,1,0:T(8,128)S(1)} %get-tuple-element.34.t1_ref, ...), custom_call_target="tpu_custom_call" | custom-call | flops 1000000000 | bytes 1916928 | tf_op jit(solution)/shard_map/pallas_call | solution.py:379
  15.2 0.9 %collective-permute-done.3.got_b_ref = f32[3,16,128]{2,1,0:T(8,128)S(1)} collective-permute-done((f32[3,16,128]{2,1,0:T(8,128)S(1)}, f32[3,16,128]{2,1,0:T(8,128)S(1)}, u32[]{:S(2)}, u32[]{:S(2)}) %collective-permute-start.3) | collective-permute-done | bytes 24608 | tf_op jit(solution)/shard_map/ppermute | solution.py:401
  16.1 0.0 collective-permute-done.4.got_a_ref
  16.1 0.0 collective-permute-done.2.got_e_ref
  16.1 1.3 %shard_map.131 = (f32[3,128,512]{2,1,0:T(8,128)}, f32[3,64,256]{2,1,0:T(8,128)}, f32[3,32,128]{2,1,0:T(8,128)}, f32[3,16,64]{2,1,0:T(8,128)}, f32[3,8,32]{2,1,0:T(8,128)}, /*index=5*/f32[3,4,16]{2,1,0:T(4,128)}) custom-call(f32[12,128,128]{2,1,0:T(8,128)S(1)} %get-tuple-element.39.g0, f32[6,64,128]{2,1,0:T(8,128)S(1)} %get-tuple-element.40.g1, ...), custom_call_target="tpu_custom_call" | custom-call | flops 100000000 | bytes 1671168 | tf_op jit(solution)/shard_map/pallas_call | solution.py:379
Async XLA Ops:
  2.2 3.8 %collective-permute-start = (f32[3,16,128]{2,1,0:T(8,128)S(1)}, f32[3,16,128]{2,1,0:T(8,128)S(1)}, u32[]{:S(2)}, u32[]{:S(2)}) collective-permute-start(f32[3,16,128]{2,1,0:T(8,128)S(1)} %get-tuple-element.29), channel_id=1, source_target_pairs={{0,8},{1,2},{2,1},{3,4},{4,3},{5,6},{6,5},{7,15},{8,0},{9,10},{10,... | collective-permute-start | bytes 73736 | tf_op jit(solution)/shard_map/ppermute | solution.py:401
  4.0 1.9 %collective-permute-start.1 = (f32[3,16,128]{2,1,0:T(8,128)S(1)}, f32[3,16,128]{2,1,0:T(8,128)S(1)}, u32[]{:S(2)}, u32[]{:S(2)}) collective-permute-start(f32[3,16,128]{2,1,0:T(8,128)S(1)} %get-tuple-element.30), channel_id=1, source_target_pairs={{0,1},{1,0},{2,3},{3,2},{4,5},{5,4},{6,7},{7,6},{8,9},{9,8},{10,11... | collective-permute-start | bytes 73736 | tf_op jit(solution)/shard_map/ppermute | solution.py:401
  6.0 8.5 %copy-start = (bf16[256,512]{1,0:T(8,128)(2,1)S(1)}, bf16[256,512]{1,0:T(8,128)(2,1)}, u32[]{:S(2)}) copy-start(bf16[256,512]{1,0:T(8,128)(2,1)} %constant.18.clone.e0) | copy-start | bytes 786436
  6.0 8.5 %copy-start.1 = (bf16[256,256]{1,0:T(8,128)(2,1)S(1)}, bf16[256,256]{1,0:T(8,128)(2,1)}, u32[]{:S(2)}) copy-start(bf16[256,256]{1,0:T(8,128)(2,1)} %constant.19.clone.e1) | copy-start | bytes 393220
  6.0 8.5 %copy-start.2 = (bf16[128,384]{1,0:T(8,128)(2,1)S(1)}, bf16[128,384]{1,0:T(8,128)(2,1)}, u32[]{:S(2)}) copy-start(bf16[128,384]{1,0:T(8,128)(2,1)} %constant.20.clone.e2) | copy-start | bytes 294916
  6.9 9.2 %collective-permute-start.4 = (f32[3,16,128]{2,1,0:T(8,128)S(1)}, f32[3,16,128]{2,1,0:T(8,128)S(1)}, u32[]{:S(2)}, u32[]{:S(2)}) collective-permute-start(f32[3,16,128]{2,1,0:T(8,128)S(1)} %get-tuple-element.44), channel_id=1, source_target_pairs={{0,8},{1,9},{2,10},{3,11},{4,12},{5,13},{6,14},{7,15},{8,0},{9,1},... | collective-permute-start | bytes 73736 | tf_op jit(solution)/shard_map/ppermute | solution.py:401
  7.7 8.4 %collective-permute-start.2 = (f32[3,16,128]{2,1,0:T(8,128)S(1)}, f32[3,16,128]{2,1,0:T(8,128)S(1)}, u32[]{:S(2)}, u32[]{:S(2)}) collective-permute-start(f32[3,16,128]{2,1,0:T(8,128)S(1)} %get-tuple-element.44), channel_id=1, source_target_pairs={{0,1},{1,0},{2,3},{3,2},{4,5},{5,4},{6,7},{7,6},{8,9},{9,8},{10,11... | collective-permute-start | bytes 73736 | tf_op jit(solution)/shard_map/ppermute | solution.py:401
  9.3 6.7 %collective-permute-start.3 = (f32[3,16,128]{2,1,0:T(8,128)S(1)}, f32[3,16,128]{2,1,0:T(8,128)S(1)}, u32[]{:S(2)}, u32[]{:S(2)}) collective-permute-start(f32[3,16,128]{2,1,0:T(8,128)S(1)} %get-tuple-element.45), channel_id=1, source_target_pairs={{0,1},{1,0},{2,3},{3,2},{4,5},{5,4},{6,7},{7,6},{8,16},{9,17},{10,... | collective-permute-start | bytes 73736 | tf_op jit(solution)/shard_map/ppermute | solution.py:401

commit v4 on v3

--- a/solution.py
+++ b/solution.py
@@ -110,14 +110,6 @@
             own[:, COPY_LANE[0]], own[:, COPY_LANE[1]] = part[m // 2], part[m // 2 + 1]
     c["col_a"] = exact(own[:, :384], 1)[0]
     c["col_b"] = np.concatenate(exact(own[:, 384:], 2), axis=1)
-    land = np.zeros((32, 512))
-    for k in range(LEVELS):
-        m = width >> (k + 1)
-        for q, at in enumerate((LOW_LANE[k], OWN_LANE[k], OWN_LANE[k] + 1)):
-            land[3 * k + q, at] = 1
-        for q, at in enumerate((OWN_LANE[k] + m - 1, HIGH_LANE[k])):
-            land[16 + 2 * k + q, at] = 1
-    c["land"] = exact(land, 1)[0]
     third = np.zeros((128, 384))
     for k in range(LEVELS):
         m = width >> (k + 1)
@@ -152,14 +144,14 @@
 
 
 def edge_kernel(
-    x_hbm, edge_hbm, a_hbm, b_hbm, land_hbm,
-    send_b_ref, send_a_ref, low_ref, high_ref, x_ref, a_ref, b_ref, land_ref,
+    x_hbm, edge_hbm, a_hbm, b_hbm,
+    send_b_ref, send_a_ref, low_ref, high_ref, x_ref, a_ref, b_ref,
     edge_ref, sems,
 ):
     channels, height, width = x_hbm.shape
     tiles = [0, width // 128 - 1, *range(1, width // 128 - 1)]
     pairs = [(edge_hbm, edge_ref)] + [(x_hbm.at[:, :, pl.ds(128 * t, 128)], x_ref.at[:, t]) for t in tiles]
-    pairs += [(a_hbm, a_ref), (b_hbm, b_ref), (land_hbm, land_ref)]
+    pairs += [(a_hbm, a_ref), (b_hbm, b_ref)]
     copies = [pltpu.make_async_copy(source, target, sems.at[i]) for i, (source, target) in enumerate(pairs)]
     for copy in copies:
         copy.start()
@@ -183,61 +175,55 @@
         copy.wait()
 
 
-def column_kernel(x_ref, a_ref, b_ref, u_ref):
-    channels, tiles, height, _ = x_ref.shape
-    x = jnp.concatenate([x_ref[:, t].reshape(channels * height, 128) for t in range(tiles)], axis=1)
-    u_ref[:, :, :384] = times(x, a_ref[...]).reshape(channels, height, 384)
-    last = times(x, b_ref[...])
-    u_ref[:, :, 384:] = (last[:, :128] + last[:, 128:]).reshape(channels, height, 128)
-
-
-def row_kernel(
-    u_ref, got_b_ref, got_a_ref, low_ref, high_ref, land_ref,
-    t1_ref, t2_ref, t3_ref, t4_ref, t5_ref, send_b_ref, send_a_ref,
-    v_ref, c1_ref, c2_ref, c3_ref, c4_ref, up_ref, down_ref,
+def padded(ref, n):
+    tiles, size = ref.shape[0], ref.shape[1]
+    ref[:, :LEAD] = jnp.zeros((tiles, LEAD, 128), F32)
+    ref[:, LEAD + n :] = jnp.zeros((tiles, size - LEAD - n, 128), F32)
+
+
+def mirrored(ref, tile, n, first, last):
+    index = lax.broadcasted_iota(jnp.int32, (8, 128), 0)
+    block = ref[tile, LEAD - 8 : LEAD]
+    near, far = ref[tile, LEAD + 1 : LEAD + 2], ref[tile, LEAD + 2 : LEAD + 3]
+    ref[tile, LEAD - 8 : LEAD] = jnp.where(first & (index == 7), near, jnp.where(first & (index == 6), far, block))
+    block = ref[tile, LEAD + n : LEAD + n + 8]
+    near = ref[tile, LEAD + n - 2 : LEAD + n - 1]
+    ref[tile, LEAD + n : LEAD + n + 8] = jnp.where(last & (index == 0), near, block)
+
+
+def reduced(ref, tile, n, first, last):
+    s = [ref[tile, pl.ds(6 + i, rows_of(n), stride=2), :] for i in range(5)]
+    r = (s[0] + s[4]) * 0.0625 + (s[1] + s[3]) * 0.25 + s[2] * 0.375
+    index = lax.broadcasted_iota(jnp.int32, r.shape, 0)
+    r = jnp.where(first & (index == 7), r[9:10], jnp.where(first & (index == 6), r[10:11], r))
+    beyond = last & (index == 8 + n)
+    return jnp.where(beyond, r[6 + n : 7 + n], r), jnp.where(beyond, r[7 + n : 8 + n], r)
+
+
+def column_kernel(
+    x_ref, a_ref, b_ref, t1_ref, t2_ref, t3_ref, t4_ref, t5_ref, up_ref, down_ref, v_ref, c1_ref, c2_ref, c3_ref, c4_ref
 ):
-    channels, height = u_ref.shape[0], u_ref.shape[1]
-    col, row = lax.axis_index("cols"), lax.axis_index("rows")
-    col_odd = col % 2 == 1
-    row_odd, first, last = row % 2 == 1, row == 0, row == lax.axis_size("rows") - 1
-    got = []
-    for ch in range(channels):
-        b, a = got_b_ref[ch], got_a_ref[ch]
-        from_left = jnp.where(col == 0, low_ref[ch], jnp.where(col_odd, a, b))
-        from_right = jnp.where(col == lax.axis_size("cols") - 1, high_ref[ch], jnp.where(col_odd, b, a))
-        got.append(jnp.concatenate([from_left, from_right], axis=0).T)
-    landed = times(jnp.concatenate(got, axis=0), land_ref[...])
-    chain = (v_ref, c1_ref, c2_ref, c3_ref, c4_ref)
+    channels, across, height, _ = x_ref.shape
+    row = lax.axis_index("rows")
+    first, last = row == 0, row == lax.axis_size("rows") - 1
+    chain, outs = (v_ref, c1_ref, c2_ref, c3_ref, c4_ref), (t1_ref, t2_ref, t3_ref, t4_ref, t5_ref)
     for k, ref in enumerate(chain):
-        n = height >> k
-        tiles, size = ref.shape[0], ref.shape[1]
-        ref[:, :LEAD] = jnp.zeros((tiles, LEAD, 128), F32)
-        ref[:, LEAD + n :] = jnp.zeros((tiles, size - LEAD - n, 128), F32)
+        padded(ref, height >> k)
+    up_ref[...] = jnp.zeros_like(up_ref)
+    down_ref[...] = jnp.zeros_like(down_ref)
+    x = jnp.concatenate([x_ref[:, t].reshape(channels * height, 128) for t in range(across)], axis=1)
+    u = times(x, a_ref[...])
+    both = times(x, b_ref[...])
+    u = jnp.concatenate([u, both[:, :128] + both[:, 128:]], axis=1)
     for ch in range(channels):
         for t in range(4):
-            lanes = slice(128 * t, 128 * (t + 1))
-            v_ref[4 * ch + t, LEAD : LEAD + height] = (
-                u_ref[ch, :, lanes] + landed[ch * height : (ch + 1) * height, lanes]
-            )
-    for tile in range(4 * channels):
-        block = v_ref[tile, LEAD - 8 : LEAD]
-        index = lax.broadcasted_iota(jnp.int32, block.shape, 0)
-        near, far = v_ref[tile, LEAD + 1 : LEAD + 2], v_ref[tile, LEAD + 2 : LEAD + 3]
-        v_ref[tile, LEAD - 8 : LEAD] = jnp.where(first, jnp.where(index == 7, near, jnp.where(index == 6, far, block)), block)
-        block = v_ref[tile, LEAD + height : LEAD + height + 8]
-        near = v_ref[tile, LEAD + height - 2 : LEAD + height - 1]
-        v_ref[tile, LEAD + height : LEAD + height + 8] = jnp.where(last & (index == 0), near, block)
-
-    up_ref[...] = jnp.zeros_like(up_ref)
-    down_ref[...] = jnp.zeros_like(down_ref)
+            v_ref[4 * ch + t, LEAD : LEAD + height] = u[ch * height : (ch + 1) * height, 128 * t : 128 * (t + 1)]
+            mirrored(v_ref, 4 * ch + t, height, first, last)
     lane = lax.broadcasted_iota(jnp.int32, (1, 128), 1) + 384
     tiles_of = ((0, 1, 2, 3), (2, 3), (3,), (3,), (3,))
-    outs = (t1_ref, t2_ref, t3_ref, t4_ref, t5_ref)
     for k in range(LEVELS):
         n = height >> (k + 1)
         count = rows_of(n)
-        source = chain[k]
-        before = tiles_of[k - 1] if k else (0, 1, 2, 3)
         mine = (lane == LOW_LANE[k]) | (lane == HIGH_LANE[k])
         if k == 0:
             mine = mine | (lane == COPY_LANE[0]) | (lane == COPY_LANE[1])
@@ -245,31 +231,85 @@
             mine = mine | (lane >= OWN_LANE[k]) & (lane < OWN_LANE[k] + (64 >> (k - 2)))
         for ch in range(channels):
             for at, t in enumerate(tiles_of[k]):
-                tile = ch * len(before) + before.index(t)
-                s = [source[tile, pl.ds(6 + i, count, stride=2), :] for i in range(5)]
-                r = (s[0] + s[4]) * 0.0625 + (s[1] + s[3]) * 0.25 + s[2] * 0.375
-                index = lax.broadcasted_iota(jnp.int32, r.shape, 0)
-                r = jnp.where(first & (index == 7), r[9:10], jnp.where(first & (index == 6), r[10:11], r))
+                onward, border = reduced(chain[k], ch * len(tiles_of[k]) + at, n, first, last)
                 if k < LEVELS - 1 and TILE_LEVELS[t] > k + 1:
-                    onward = jnp.where(last & (index == 8 + n), r[6 + n : 7 + n], r)
-                    chain[k + 1][ch * len(tiles_of[k]) + at, LEAD - 8 : LEAD - 8 + count] = onward
+                    chain[k + 1][ch * len(tiles_of[k + 1]) + tiles_of[k + 1].index(t), LEAD - 8 : LEAD - 8 + count] = onward
                 if t in TILES[k]:
-                    border = jnp.where(last & (index == 8 + n), r[7 + n : 8 + n], r)
                     outs[k][ch * len(TILES[k]) + TILES[k].index(t)] = border
-                    going_up, going_down = r[7:9], r[7 + n : 10 + n]
+                    going_up, going_down = border[7:9], border[7 + n : 10 + n]
                     if t == 3:
                         going_up = jnp.where(mine, going_up, 0.0) + (up_ref[ch, 12:14] if k else 0.0)
                         going_down = jnp.where(mine, going_down, 0.0) + (down_ref[ch, 12:15] if k else 0.0)
                     up_ref[ch, 4 * t : 4 * t + 2] = going_up
                     down_ref[ch, 4 * t : 4 * t + 3] = going_down
+
+
+def landed(cells, k, ch, width):
+    lane = lax.broadcasted_iota(jnp.int32, cells.shape, 1)
+    w = width >> (k + 1)
+    out = {}
+    for source, target, run in (
+        (3 * k, LOW_LANE[k], 1),
+        (3 * k + 1, OWN_LANE[k], 2),
+        (16 + 2 * k, OWN_LANE[k] + w - 1, 1),
+        (17 + 2 * k, HIGH_LANE[k], 1),
+    ):
+        tile, at = target // 128, target % 128
+        moved = pltpu.roll(cells, (at - 32 * ch - source) % 128, 1)
+        out[tile] = jnp.where((lane >= at) & (lane < at + run), moved, out.get(tile, 0.0))
+    return out
+
+
+def row_kernel(
+    got_b_ref, got_a_ref, low_ref, high_ref, own_up_ref, own_down_ref,
+    send_b_ref, send_a_ref, p1_ref, p2_ref, p3_ref, p4_ref, p5_ref,
+    v_ref, c1_ref, c2_ref, c3_ref, c4_ref, up_ref, down_ref,
+):
+    channels, height = got_b_ref.shape[0], got_b_ref.shape[2]
+    col, row = lax.axis_index("cols"), lax.axis_index("rows")
+    col_odd = col % 2 == 1
+    row_odd, first, last = row % 2 == 1, row == 0, row == lax.axis_size("rows") - 1
+    chain, outs = (v_ref, c1_ref, c2_ref, c3_ref, c4_ref), (p1_ref, p2_ref, p3_ref, p4_ref, p5_ref)
+    for k, ref in enumerate(chain):
+        padded(ref, height >> k)
+    got = []
+    for ch in range(channels):
+        b, a = got_b_ref[ch], got_a_ref[ch]
+        got.append(jnp.where(col == 0, low_ref[ch], jnp.where(col_odd, a, b)))
+        got.append(jnp.where(col == lax.axis_size("cols") - 1, high_ref[ch], jnp.where(col_odd, b, a)))
+    got.append(jnp.zeros((128 - 32 * channels, height), F32))
+    v_ref[0, LEAD : LEAD + height] = jnp.concatenate(got, axis=0).T
+    mirrored(v_ref, 0, height, first, last)
+    up_ref[...] = own_up_ref[...]
+    down_ref[...] = own_down_ref[...]
+    for k in range(LEVELS):
+        n = height >> (k + 1)
+        onward, border = reduced(chain[k], 0, n, first, last)
+        if k < LEVELS - 1:
+            chain[k + 1][0, LEAD - 8 : LEAD - 8 + rows_of(n)] = onward
+        outs[k][...] = border
+        ends = jnp.concatenate([border[:16], border[n : n + 16]], axis=0)
+        for ch in range(channels):
+            for t, add in landed(ends, k, ch, 128 * 4).items():
+                up_ref[ch, 4 * t : 4 * t + 2] = up_ref[ch, 4 * t : 4 * t + 2] + add[7:9]
+                down_ref[ch, 4 * t : 4 * t + 3] = down_ref[ch, 4 * t : 4 * t + 3] + add[23:26]
     send_b_ref[...] = jnp.where(row_odd, down_ref[...], up_ref[...])
     send_a_ref[...] = jnp.where(row_odd, up_ref[...], down_ref[...])
 
 
-def own_kernel(x_ref, t1_ref, t2_ref, t3_ref, t4_ref, t5_ref, e0, e1, e2, g0, g1, g2, g3, g4, y1, y2, y3, y4, y5):
-    channels, _, height, _ = x_ref.shape
-    levels, owns, ys = (t1_ref, t2_ref, t3_ref, t4_ref, t5_ref), (g0, g1, g2, g3, g4), (y1, y2, y3, y4, y5)
+def own_kernel(
+    x_ref, t1_ref, t2_ref, t3_ref, t4_ref, t5_ref, p1_ref, p2_ref, p3_ref, p4_ref, p5_ref, e0, e1, e2,
+    g0, g1, g2, g3, g4, s5, s1, s2, s3, s4, y1, y2, y3, y4, y5,
+):
+    channels, wide, height, _ = x_ref.shape
+    levels, owns, ys = (s1, s2, s3, s4, s5), (g0, g1, g2, g3, g4), (y1, y2, y3, y4, y5)
+    own_sums, received = (t1_ref, t2_ref, t3_ref, t4_ref, t5_ref), (p1_ref, p2_ref, p3_ref, p4_ref, p5_ref)
     for k in range(LEVELS):
+        for ch in range(channels):
+            add = landed(received[k][...], k, ch, 128 * wide)
+            for at, t in enumerate(TILES[k]):
+                tile = ch * len(TILES[k]) + at
+                levels[k][tile] = own_sums[k][tile] + add[t]
         n, count, tiles = height >> (k + 1), levels[k].shape[1], len(TILES[k])
         cells = levels[k][...].reshape(channels, tiles, count, 128)
         cells = [cells[:, at].reshape(channels * count, 128) for at in range(tiles)]
@@ -295,7 +335,7 @@
 
 
 def early(row):
-    return (row % 8 == 2) | ((row % 8 == 0) & (row > 0))
+    return (row % 8 == 0) & (row > 0)
 
 
 def end_kernel(
@@ -405,49 +445,56 @@
     channels, height, width = x.shape
     c = {name: jnp.asarray(value) for name, value in constants(width).items()}
     side = (channels, 16, height)
-    fixed = [c[name] for name in ("edge", "col_a", "col_b", "land")]
-    send_b, send_a, low, high, x_near, col_a, col_b, land = call(
+    fixed = [c[name] for name in ("edge", "col_a", "col_b")]
+    send_b, send_a, low, high, x_near, col_a, col_b = call(
         edge_kernel,
         [side] * 4 + [(channels, width // 128, height, 128)] + [(a.shape, BF16) for a in fixed[1:]],
         10**8,
         [pltpu.with_memory_space_constraint(a, pltpu.HBM) for a in (x, *fixed)],
-        [pltpu.VMEM(c["edge"].shape, BF16), pltpu.SemaphoreType.DMA((8,))],
+        [pltpu.VMEM(c["edge"].shape, BF16), pltpu.SemaphoreType.DMA((7,))],
         HBM,
     )
     rows, cols = lax.axis_size("rows"), lax.axis_size("cols")
     pairs = lambda first, count: [(i, i + 1) for i in range(first, count - 1, 2)]
     got_b = swap(send_b, "cols", pairs(1, cols), lambda r, c: (r ^ 1, c))
     got_a = swap(send_a, "cols", pairs(0, cols), None)
-    (u,) = call(column_kernel, [(channels, height, 512)], 10**9, (x_near, col_a, col_b))
     ns = [height >> (k + 1) for k in range(LEVELS)]
-    tall = lambda tiles, n: pltpu.VMEM((tiles * channels, LEAD + n + TAIL, 128), F32)
+    tall = lambda tiles: [pltpu.VMEM((t, LEAD + n + TAIL, 128), F32) for t, n in zip(tiles, (height, *ns))]
     message = (channels, 16, 128)
-    *t, send_b, send_a = call(
+    sums = [(channels * len(t), rows_of(n), 128) for n, t in zip(ns, TILES)]
+    *t, up, down = call(
+        column_kernel,
+        sums + [message] * 2,
+        10**9,
+        (x_near, col_a, col_b),
+        tall([channels * count for count in (4, 2, 1, 1, 1)]),
+    )
+    send_b, send_a, *p = call(
         row_kernel,
-        [(channels * len(t), rows_of(n), 128) for n, t in zip(ns, TILES)] + [message] * 2,
-        10**8,
-        (u, got_b, got_a, low, high, land),
-        [tall(4, height), tall(4, ns[0]), tall(2, ns[1]), tall(1, ns[2]), tall(1, ns[3])]
-        + [pltpu.VMEM(message, F32)] * 2,
+        [message] * 2 + [(rows_of(n), 128) for n in ns],
+        10**7,
+        (got_b, got_a, low, high, up, down),
+        tall([1] * 5) + [pltpu.VMEM(message, F32)] * 2,
     )
     beside = lambda r, c: (r, c ^ 1)
     got_e = swap(send_a, "rows", [p for p in pairs(0, rows) if early(p[0])], beside)
     got_b = swap(send_b, "rows", pairs(1, rows), beside)
     got_a = swap(send_a, "rows", [p for p in pairs(0, rows) if not early(p[0])], beside)
     expand = [c[f"expand_{k}"] for k in range(3)]
-    own = call(
+    *own, coarse = call(
         own_kernel,
-        [(channels * max(1, width >> (k + 7)), height >> k, 128) for k in range(LEVELS)],
+        [(channels * max(1, width >> (k + 7)), height >> k, 128) for k in range(LEVELS)] + sums[-1:],
         10**9,
-        (x_near, *t, *expand),
-        [pltpu.VMEM((channels, rows_of(n), max(128, width >> k)), F32) for k, n in enumerate(ns)],
+        (x_near, *t, *p, *expand),
+        [pltpu.VMEM(s, F32) for s in sums[:-1]]
+        + [pltpu.VMEM((channels, rows_of(n), max(128, width >> k)), F32) for k, n in enumerate(ns)],
     )
     outs = [(channels, height >> k, width >> k) for k in range(LEVELS + 1)]
     return call(
         end_kernel,
         outs,
         10**8,
-        (*own, t[-1], got_e, got_b, got_a, *expand),
+        (*own, coarse, got_e, got_b, got_a, *expand),
         [pltpu.VMEM((channels, 8, s[2]), F32) for s in outs[:3] for _ in range(2)]
         + [pltpu.VMEM(s, F32) for s in outs[3:]]
         + [pltpu.SemaphoreType.DMA((30,))],

time: 17.5 us -> 17 us (0.971)
  starting transfers between devices: 10.3 us -> 10 us
    ppermute x5, starting transfers between devices: 10.3 us -> 10 us  [swap(): return lax.ppermute(x, ('rows', 'cols'), list(enumerate(to)))]
  transfers between devices with their start and end apart: 5 -> 5, of which waited for: 1 -> 1; matrix products, arithmetic and copies ran while one was open for 0% -> 0% of each run, Pallas kernels for 10% -> 12%
where the time goes in v4:
time: 17 us; the launch traced here: 16.9 us
  starting transfers between devices  10 us (59%)
  Pallas kernels  5.35 us (31%)
  waiting for transfers between devices  0.85 us (5%)
  between operations  0.69 us (4%)
    ppermute x5, starting transfers between devices, swap(): return lax.ppermute(x, ('rows', 'cols'), list(enumerate(to)))  10 us
    pallas_call x5, Pallas kernels, call(): pl.pallas_call(kernel, out_shape=outs, in_specs=[in_space] * len(args), o...  5.35 us
    ppermute x5, waiting for transfers between devices, swap(): return lax.ppermute(x, ('rows', 'cols'), list(enumerate(to)))  0.85 us
  transfers between devices with their start and end apart: 5, of which 1 were waited for; matrix products, arithmetic and copies ran while one was open for 0% of the time, Pallas kernels for 12%

profile of v4, /device:TPU:25, one launch (start us, length us, event | category | flops | bytes accessed | tf_op | source)
XLA Modules:
  0.0 16.9 jit_solution(14452290269241976767)
XLA Ops:
  0.6 1.5 %shard_map.118 = (f32[3,16,128]{2,1,0:T(8,128)S(1)}, f32[3,16,128]{2,1,0:T(8,128)S(1)}, f32[3,16,128]{2,1,0:T(8,128)S(1)}, f32[3,16,128]{2,1,0:T(8,128)S(1)}, f3...) custom-call(f32[3,128,512]{2,1,0:T(8,128)} %x_hbm.1, ...), custom_call_target="tpu_custom_call" | custom-call | flops 100000000 | bytes 1474560 | tf_op jit(solution)/shard_map/pallas_call | solution.py:419
  2.2 1.9 %collective-permute-start = (f32[3,16,128]{2,1,0:T(8,128)S(1)}, f32[3,16,128]{2,1,0:T(8,128)S(1)}, u32[]{:S(2)}, u32[]{:S(2)}) collective-permute-start(f32[3,16,128]{2,1,0:T(8,128)S(1)} %get-tuple-element.41), channel_id=1, source_target_pairs={{0,8},{1,2},{2,1},{3,4},{4,3},{5,6},{6,5},{7,15},{8,0},{9,10},{10,... | collective-permute-start | bytes 73736 | tf_op jit(solution)/shard_map/ppermute | solution.py:441
  4.0 0.8 %collective-permute-start.1 = (f32[3,16,128]{2,1,0:T(8,128)S(1)}, f32[3,16,128]{2,1,0:T(8,128)S(1)}, u32[]{:S(2)}, u32[]{:S(2)}) collective-permute-start(f32[3,16,128]{2,1,0:T(8,128)S(1)} %get-tuple-element.42), channel_id=1, source_target_pairs={{0,1},{1,0},{2,3},{3,2},{4,5},{5,4},{6,7},{7,6},{8,9},{9,8},{10,11... | collective-permute-start | bytes 73736 | tf_op jit(solution)/shard_map/ppermute | solution.py:441
  4.8 0.0 copy-start
  4.8 0.0 copy-start.2
  4.8 1.4 %shard_map.119 = (f32[9,80,128]{2,1,0:T(8,128)S(1)}, f32[6,48,128]{2,1,0:T(8,128)S(1)}, f32[3,32,128]{2,1,0:T(8,128)S(1)}, f32[3,24,128]{2,1,0:T(8,128)S(1)}, f3...) custom-call(f32[3,4,128,128]{3,2,1,0:T(8,128)S(1)} %get-tuple-element.33.x_ref, ...), custom_call_target="tpu_custom_call" | custom-call | flops 1000000000 | bytes 1441792 | tf_op jit(solution)/shard_map/pallas_call | solution.py:419
  6.2 0.0 copy-start.1
  6.2 0.0 collective-permute-done.got_b_ref
  6.2 0.0 collective-permute-done.1.got_a_ref
  6.2 0.5 %shard_map.120 = (f32[3,16,128]{2,1,0:T(8,128)S(1)}, f32[3,16,128]{2,1,0:T(8,128)S(1)}, f32[80,128]{1,0:T(8,128)S(1)}, f32[48,128]{1,0:T(8,128)S(1)}, f32[32,128...) custom-call(f32[3,16,128]{2,1,0:T(8,128)S(1)} %collective-permute-done.got_b_ref, ...), custom_call_target="tpu_custom_call" | custom-call | flops 10000000 | bytes 147456 | tf_op jit(solution)/shard_map/pallas_call | solution.py:419
  6.7 0.6 %collective-permute-start.4 = (f32[3,16,128]{2,1,0:T(8,128)S(1)}, f32[3,16,128]{2,1,0:T(8,128)S(1)}, u32[]{:S(2)}, u32[]{:S(2)}) collective-permute-start(f32[3,16,128]{2,1,0:T(8,128)S(1)} %get-tuple-element.58), channel_id=1, source_target_pairs={{0,8},{1,9},{2,10},{3,11},{4,12},{5,13},{6,14},{7,15},{8,0},{9,1},... | collective-permute-start | bytes 73736 | tf_op jit(solution)/shard_map/ppermute | solution.py:441
  7.3 1.6 %collective-permute-start.2 = (f32[3,16,128]{2,1,0:T(8,128)S(1)}, f32[3,16,128]{2,1,0:T(8,128)S(1)}, u32[]{:S(2)}, u32[]{:S(2)}) collective-permute-start(f32[3,16,128]{2,1,0:T(8,128)S(1)} %get-tuple-element.58), channel_id=1, source_target_pairs={{0,1},{1,0},{2,3},{3,2},{4,5},{5,4},{6,7},{7,6},{8,9},{9,8},{10,11... | collective-permute-start | bytes 73736 | tf_op jit(solution)/shard_map/ppermute | solution.py:441
  8.9 5.1 %collective-permute-start.3 = (f32[3,16,128]{2,1,0:T(8,128)S(1)}, f32[3,16,128]{2,1,0:T(8,128)S(1)}, u32[]{:S(2)}, u32[]{:S(2)}) collective-permute-start(f32[3,16,128]{2,1,0:T(8,128)S(1)} %get-tuple-element.59), channel_id=1, source_target_pairs={{0,1},{1,0},{2,3},{3,2},{4,5},{5,4},{6,7},{7,6},{8,16},{9,17},{10,... | collective-permute-start | bytes 73736 | tf_op jit(solution)/shard_map/ppermute | solution.py:441
  14.1 0.0 copy-done
  14.1 0.0 copy-done.2
  14.1 0.0 copy-done.1
  14.1 0.7 %shard_map.121 = (f32[12,128,128]{2,1,0:T(8,128)S(1)}, f32[6,64,128]{2,1,0:T(8,128)S(1)}, f32[3,32,128]{2,1,0:T(8,128)S(1)}, f32[3,16,128]{2,1,0:T(8,128)S(1)}, ...) custom-call(f32[3,4,128,128]{3,2,1,0:T(8,128)S(1)} %get-tuple-element.33.x_ref, ...), custom_call_target="tpu_custom_call" | custom-call | flops 1000000000 | bytes 2023424 | tf_op jit(solution)/shard_map/pallas_call | solution.py:419
  14.8 0.8 %collective-permute-done.3.got_b_ref = f32[3,16,128]{2,1,0:T(8,128)S(1)} collective-permute-done((f32[3,16,128]{2,1,0:T(8,128)S(1)}, f32[3,16,128]{2,1,0:T(8,128)S(1)}, u32[]{:S(2)}, u32[]{:S(2)}) %collective-permute-start.3) | collective-permute-done | bytes 24608 | tf_op jit(solution)/shard_map/ppermute | solution.py:441
  15.7 0.0 collective-permute-done.4.got_a_ref
  15.7 0.0 collective-permute-done.2.got_e_ref
  15.7 1.3 %shard_map.122 = (f32[3,128,512]{2,1,0:T(8,128)}, f32[3,64,256]{2,1,0:T(8,128)}, f32[3,32,128]{2,1,0:T(8,128)}, f32[3,16,64]{2,1,0:T(8,128)}, f32[3,8,32]{2,1,0:T(8,128)}, /*index=5*/f32[3,4,16]{2,1,0:T(4,128)}) custom-call(f32[12,128,128]{2,1,0:T(8,128)S(1)} %get-tuple-element.52.g0, f32[6,64,128]{2,1,0:T(8,128)S(1)} %get-tuple-element.53.g1, ...), custom_call_target="tpu_custom_call" | custom-call | flops 100000000 | bytes 1671168 | tf_op jit(solution)/shard_map/pallas_call | solution.py:419
Async XLA Ops:
  2.2 4.1 %collective-permute-start = (f32[3,16,128]{2,1,0:T(8,128)S(1)}, f32[3,16,128]{2,1,0:T(8,128)S(1)}, u32[]{:S(2)}, u32[]{:S(2)}) collective-permute-start(f32[3,16,128]{2,1,0:T(8,128)S(1)} %get-tuple-element.41), channel_id=1, source_target_pairs={{0,8},{1,2},{2,1},{3,4},{4,3},{5,6},{6,5},{7,15},{8,0},{9,10},{10,... | collective-permute-start | bytes 73736 | tf_op jit(solution)/shard_map/ppermute | solution.py:441
  4.0 2.2 %collective-permute-start.1 = (f32[3,16,128]{2,1,0:T(8,128)S(1)}, f32[3,16,128]{2,1,0:T(8,128)S(1)}, u32[]{:S(2)}, u32[]{:S(2)}) collective-permute-start(f32[3,16,128]{2,1,0:T(8,128)S(1)} %get-tuple-element.42), channel_id=1, source_target_pairs={{0,1},{1,0},{2,3},{3,2},{4,5},{5,4},{6,7},{7,6},{8,9},{9,8},{10,11... | collective-permute-start | bytes 73736 | tf_op jit(solution)/shard_map/ppermute | solution.py:441
  4.8 9.2 %copy-start = (bf16[256,512]{1,0:T(8,128)(2,1)S(1)}, bf16[256,512]{1,0:T(8,128)(2,1)}, u32[]{:S(2)}) copy-start(bf16[256,512]{1,0:T(8,128)(2,1)} %constant.15.clone.e0) | copy-start | bytes 786436
  4.8 9.2 %copy-start.2 = (bf16[128,384]{1,0:T(8,128)(2,1)S(1)}, bf16[128,384]{1,0:T(8,128)(2,1)}, u32[]{:S(2)}) copy-start(bf16[128,384]{1,0:T(8,128)(2,1)} %constant.17.clone.e2) | copy-start | bytes 294916
  6.2 7.9 %copy-start.1 = (bf16[256,256]{1,0:T(8,128)(2,1)S(1)}, bf16[256,256]{1,0:T(8,128)(2,1)}, u32[]{:S(2)}) copy-start(bf16[256,256]{1,0:T(8,128)(2,1)} %constant.16.clone.e1) | copy-start | bytes 393220
  6.7 8.9 %collective-permute-start.4 = (f32[3,16,128]{2,1,0:T(8,128)S(1)}, f32[3,16,128]{2,1,0:T(8,128)S(1)}, u32[]{:S(2)}, u32[]{:S(2)}) collective-permute-start(f32[3,16,128]{2,1,0:T(8,128)S(1)} %get-tuple-element.58), channel_id=1, source_target_pairs={{0,8},{1,9},{2,10},{3,11},{4,12},{5,13},{6,14},{7,15},{8,0},{9,1},... | collective-permute-start | bytes 73736 | tf_op jit(solution)/shard_map/ppermute | solution.py:441
  7.3 8.4 %collective-permute-start.2 = (f32[3,16,128]{2,1,0:T(8,128)S(1)}, f32[3,16,128]{2,1,0:T(8,128)S(1)}, u32[]{:S(2)}, u32[]{:S(2)}) collective-permute-start(f32[3,16,128]{2,1,0:T(8,128)S(1)} %get-tuple-element.58), channel_id=1, source_target_pairs={{0,1},{1,0},{2,3},{3,2},{4,5},{5,4},{6,7},{7,6},{8,9},{9,8},{10,11... | collective-permute-start | bytes 73736 | tf_op jit(solution)/shard_map/ppermute | solution.py:441
  8.9 6.7 %collective-permute-start.3 = (f32[3,16,128]{2,1,0:T(8,128)S(1)}, f32[3,16,128]{2,1,0:T(8,128)S(1)}, u32[]{:S(2)}, u32[]{:S(2)}) collective-permute-start(f32[3,16,128]{2,1,0:T(8,128)S(1)} %get-tuple-element.59), channel_id=1, source_target_pairs={{0,1},{1,0},{2,3},{3,2},{4,5},{5,4},{6,7},{7,6},{8,16},{9,17},{10,... | collective-permute-start | bytes 73736 | tf_op jit(solution)/shard_map/ppermute | solution.py:441

commit v5 on v4

--- a/solution.py
+++ b/solution.py
@@ -81,6 +81,9 @@
 COPY_LANE = (506, 507)
 TILES = ((0, 1, 3), (2, 3), (3,), (3,), (3,))
 TILE_LEVELS = (1, 1, 2, 5)
+MESSAGE = (32, 128)
+MESSAGE_ROW = (0, 2, 4, 7)
+MESSAGE_ROWS = (2, 2, 3, 3)
 LEAD = 24
 TAIL = 32
 
@@ -236,18 +239,18 @@
                     chain[k + 1][ch * len(tiles_of[k + 1]) + tiles_of[k + 1].index(t), LEAD - 8 : LEAD - 8 + count] = onward
                 if t in TILES[k]:
                     outs[k][ch * len(TILES[k]) + TILES[k].index(t)] = border
-                    going_up, going_down = border[7:9], border[7 + n : 10 + n]
+                    at_row, rows = 10 * ch + MESSAGE_ROW[t], MESSAGE_ROWS[t]
+                    going_up, going_down = border[7:9], border[7 + n : 7 + n + rows]
                     if t == 3:
-                        going_up = jnp.where(mine, going_up, 0.0) + (up_ref[ch, 12:14] if k else 0.0)
-                        going_down = jnp.where(mine, going_down, 0.0) + (down_ref[ch, 12:15] if k else 0.0)
-                    up_ref[ch, 4 * t : 4 * t + 2] = going_up
-                    down_ref[ch, 4 * t : 4 * t + 3] = going_down
-
-
-def landed(cells, k, ch, width):
+                        going_up = jnp.where(mine, going_up, 0.0) + (up_ref[at_row : at_row + 2] if k else 0.0)
+                        going_down = jnp.where(mine, going_down, 0.0) + (down_ref[at_row : at_row + rows] if k else 0.0)
+                    up_ref[at_row : at_row + 2] = going_up
+                    down_ref[at_row : at_row + rows] = going_down
+
+
+def landed(cells, k, ch, width, out):
     lane = lax.broadcasted_iota(jnp.int32, cells.shape, 1)
     w = width >> (k + 1)
-    out = {}
     for source, target, run in (
         (3 * k, LOW_LANE[k], 1),
         (3 * k + 1, OWN_LANE[k], 2),
@@ -282,17 +285,24 @@
     mirrored(v_ref, 0, height, first, last)
     up_ref[...] = own_up_ref[...]
     down_ref[...] = own_down_ref[...]
+    r = lax.broadcasted_iota(jnp.int32, (8, 128), 0)
+    tops, lows = [{} for _ in range(channels)], [{} for _ in range(channels)]
     for k in range(LEVELS):
         n = height >> (k + 1)
         onward, border = reduced(chain[k], 0, n, first, last)
         if k < LEVELS - 1:
             chain[k + 1][0, LEAD - 8 : LEAD - 8 + rows_of(n)] = onward
         outs[k][...] = border
-        ends = jnp.concatenate([border[:16], border[n : n + 16]], axis=0)
+        top = jnp.where(r == 7, border[:8], border[8:16])
+        low = jnp.where(r == 7, border[n : n + 8], border[n + 8 : n + 16]) if n % 8 == 0 else pltpu.roll(border[8:16], 4, 0)
         for ch in range(channels):
-            for t, add in landed(ends, k, ch, 128 * 4).items():
-                up_ref[ch, 4 * t : 4 * t + 2] = up_ref[ch, 4 * t : 4 * t + 2] + add[7:9]
-                down_ref[ch, 4 * t : 4 * t + 3] = down_ref[ch, 4 * t : 4 * t + 3] + add[23:26]
+            landed(top, k, ch, 128 * 4, tops[ch])
+            landed(low, k, ch, 128 * 4, lows[ch])
+    for ch in range(channels):
+        for t in range(4):
+            at, rows = 10 * ch + MESSAGE_ROW[t], MESSAGE_ROWS[t]
+            up_ref[at : at + 2] = up_ref[at : at + 2] + pltpu.roll(tops[ch][t], 1, 0)[:2]
+            down_ref[at : at + rows] = down_ref[at : at + rows] + pltpu.roll(lows[ch][t], 1, 0)[:rows]
     send_b_ref[...] = jnp.where(row_odd, down_ref[...], up_ref[...])
     send_a_ref[...] = jnp.where(row_odd, up_ref[...], down_ref[...])
 
@@ -306,7 +316,7 @@
     own_sums, received = (t1_ref, t2_ref, t3_ref, t4_ref, t5_ref), (p1_ref, p2_ref, p3_ref, p4_ref, p5_ref)
     for k in range(LEVELS):
         for ch in range(channels):
-            add = landed(received[k][...], k, ch, 128 * wide)
+            add = landed(received[k][...], k, ch, 128 * wide, {})
             for at, t in enumerate(TILES[k]):
                 tile = ch * len(TILES[k]) + at
                 levels[k][tile] = own_sums[k][tile] + add[t]
@@ -343,7 +353,7 @@
     d0_hbm, d1_hbm, d2_hbm, d3_hbm, d4_hbm, coarsest_hbm,
     top0, low0, top1, low1, top2, low2, n3, n4, n5, sems,
 ):
-    channels = got_b_ref.shape[0]
+    channels = n3.shape[0]
     row = lax.axis_index("rows")
     odd = row % 2 == 1
     first, last = row == 0, row == lax.axis_size("rows") - 1
@@ -368,17 +378,17 @@
     to_top = (weights((0, 0.125)), weights((0, 0.75), (1, 0.5), (2, 0.125)), weights((0, 0.125), (1, 0.5), (2, 0.75), (3, 0.5), (4, 0.125)))
     to_low = (weights((4, 0.125), (5, 0.5), (6, 0.75), (7, 0.5)), weights((6, 0.125), (7, 0.5)))
     coarse, fine = [[] for _ in range(4)], []
+    b, a = got_b_ref[...], jnp.where(early(row - row % 2), got_e_ref[...], got_a_ref[...])
+    from_up, from_down = jnp.where(first, 0.0, jnp.where(odd, a, b)), jnp.where(last, 0.0, jnp.where(odd, b, a))
     for ch in range(channels):
         fine.append([])
-        b, a = got_b_ref[ch], jnp.where(early(row - row % 2), got_e_ref[ch], got_a_ref[ch])
-        from_up, from_down = jnp.where(first, 0.0, jnp.where(odd, a, b)), jnp.where(last, 0.0, jnp.where(odd, b, a))
         for t in range(4):
-            up, down = from_up[4 * t : 4 * t + 3], from_down[4 * t : 4 * t + 2]
-            coarse[t].append(sum(w * up[i : i + 1] for i, w in enumerate(to_top)))
+            at, rows = 10 * ch + MESSAGE_ROW[t], MESSAGE_ROWS[t]
+            up, down = from_up[at : at + rows], from_down[at : at + 2]
+            coarse[t].append(sum(w * up[i : i + 1] for i, w in enumerate(to_top[:rows])))
             coarse[t].append(sum(w * down[i : i + 1] for i, w in enumerate(to_low)))
-            fine[ch].append(
-                (jnp.where(r == 0, up[1:2], jnp.where(r == 1, up[2:3], 0.0)), jnp.where(r == 7, down[:1], 0.0), down[:1])
-            )
+            top = jnp.where(r == 0, up[1:2], jnp.where(r == 1, up[2:3], 0.0) if rows > 2 else 0.0)
+            fine[ch].append((top, jnp.where(r == 7, down[:1], 0.0), down[:1]))
     coarse = [jnp.concatenate(tiles, axis=0) for tiles in coarse]
     e = [times(jnp.concatenate([coarse[half], coarse[3]], axis=1), e0[:, 256 * half : 256 * half + 256]) for half in range(2)]
     e.append(times(jnp.concatenate([coarse[2], coarse[3]], axis=1), e1[...]))
@@ -460,21 +470,20 @@
     got_a = swap(send_a, "cols", pairs(0, cols), None)
     ns = [height >> (k + 1) for k in range(LEVELS)]
     tall = lambda tiles: [pltpu.VMEM((t, LEAD + n + TAIL, 128), F32) for t, n in zip(tiles, (height, *ns))]
-    message = (channels, 16, 128)
     sums = [(channels * len(t), rows_of(n), 128) for n, t in zip(ns, TILES)]
     *t, up, down = call(
         column_kernel,
-        sums + [message] * 2,
+        sums + [MESSAGE] * 2,
         10**9,
         (x_near, col_a, col_b),
         tall([channels * count for count in (4, 2, 1, 1, 1)]),
     )
     send_b, send_a, *p = call(
         row_kernel,
-        [message] * 2 + [(rows_of(n), 128) for n in ns],
+        [MESSAGE] * 2 + [(rows_of(n), 128) for n in ns],
         10**7,
         (got_b, got_a, low, high, up, down),
-        tall([1] * 5) + [pltpu.VMEM(message, F32)] * 2,
+        tall([1] * 5) + [pltpu.VMEM(MESSAGE, F32)] * 2,
     )
     beside = lambda r, c: (r, c ^ 1)
     got_e = swap(send_a, "rows", [p for p in pairs(0, rows) if early(p[0])], beside)

time: 17 us -> 16.7 us (0.982)
  the two profiles are of different devices: /device:TPU:25 before, /device:TPU:24 now
where the time goes in v5:
time: 16.7 us; the launch traced here: 16.6 us
  starting transfers between devices  9.13 us (55%)
  Pallas kernels  5.22 us (31%)
  waiting for transfers between devices  1.5 us (9%)
  between operations  0.68 us (4%)
    ppermute x5, starting transfers between devices, swap(): return lax.ppermute(x, ('rows', 'cols'), list(enumerate(to)))  9.13 us
    pallas_call x5, Pallas kernels, call(): pl.pallas_call(kernel, out_shape=outs, in_specs=[in_space] * len(args), o...  5.22 us
    ppermute x5, waiting for transfers between devices, swap(): return lax.ppermute(x, ('rows', 'cols'), list(enumerate(to)))  1.5 us
  transfers between devices with their start and end apart: 5, of which 2 were waited for; matrix products, arithmetic and copies ran while one was open for 0% of the time, Pallas kernels for 13%

profile of v5, /device:TPU:24, one launch (start us, length us, event | category | flops | bytes accessed | tf_op | source)
XLA Modules:
  0.0 16.6 jit_solution(5415595948931491895)
XLA Ops:
  0.6 1.5 %shard_map.118 = (f32[3,16,128]{2,1,0:T(8,128)S(1)}, f32[3,16,128]{2,1,0:T(8,128)S(1)}, f32[3,16,128]{2,1,0:T(8,128)S(1)}, f32[3,16,128]{2,1,0:T(8,128)S(1)}, f3...) custom-call(f32[3,128,512]{2,1,0:T(8,128)} %x_hbm.1, ...), custom_call_target="tpu_custom_call" | custom-call | flops 100000000 | bytes 1474560 | tf_op jit(solution)/shard_map/pallas_call | solution.py:429
  2.2 2.0 %collective-permute-start = (f32[3,16,128]{2,1,0:T(8,128)S(1)}, f32[3,16,128]{2,1,0:T(8,128)S(1)}, u32[]{:S(2)}, u32[]{:S(2)}) collective-permute-start(f32[3,16,128]{2,1,0:T(8,128)S(1)} %get-tuple-element.41), channel_id=1, source_target_pairs={{0,8},{1,2},{2,1},{3,4},{4,3},{5,6},{6,5},{7,15},{8,0},{9,10},{10,... | collective-permute-start | bytes 73736 | tf_op jit(solution)/shard_map/ppermute | solution.py:451
  4.2 0.0 collective-permute-start.1
  4.2 0.0 copy-start
  4.2 0.0 copy-start.2
  4.2 1.4 %shard_map.119 = (f32[9,80,128]{2,1,0:T(8,128)S(1)}, f32[6,48,128]{2,1,0:T(8,128)S(1)}, f32[3,32,128]{2,1,0:T(8,128)S(1)}, f32[3,24,128]{2,1,0:T(8,128)S(1)}, f3...) custom-call(f32[3,4,128,128]{3,2,1,0:T(8,128)S(1)} %get-tuple-element.33.x_ref, ...), custom_call_target="tpu_custom_call" | custom-call | flops 1000000000 | bytes 1441792 | tf_op jit(solution)/shard_map/pallas_call | solution.py:429
  5.5 0.0 copy-start.1
  5.5 0.5 %collective-permute-done.got_b_ref = f32[3,16,128]{2,1,0:T(8,128)S(1)} collective-permute-done((f32[3,16,128]{2,1,0:T(8,128)S(1)}, f32[3,16,128]{2,1,0:T(8,128)S(1)}, u32[]{:S(2)}, u32[]{:S(2)}) %collective-permute-start) | collective-permute-done | bytes 24608 | tf_op jit(solution)/shard_map/ppermute | solution.py:451
  6.1 0.0 collective-permute-done.1.got_a_ref
  6.1 0.3 %shard_map.120 = (f32[32,128]{1,0:T(8,128)S(1)}, f32[32,128]{1,0:T(8,128)S(1)}, f32[80,128]{1,0:T(8,128)S(1)}, f32[48,128]{1,0:T(8,128)S(1)}, f32[32,128]{1,0:T(...) custom-call(f32[3,16,128]{2,1,0:T(8,128)S(1)} %collective-permute-done.got_b_ref, ...), custom_call_target="tpu_custom_call" | custom-call | flops 10000000 | bytes 131072 | tf_op jit(solution)/shard_map/pallas_call | solution.py:429
  6.4 0.1 collective-permute-start.4
  6.5 2.0 %collective-permute-start.2 = (f32[32,128]{1,0:T(8,128)S(1)}, f32[32,128]{1,0:T(8,128)S(1)}, u32[]{:S(2)}, u32[]{:S(2)}) collective-permute-start(f32[32,128]{1,0:T(8,128)S(1)} %get-tuple-element.58), channel_id=1, source_target_pairs={{0,1},{1,0},{2,3},{3,2},{4,5},{5,4},{6,7},{7,6},{8,9},{9,8},{10,11... | collective-permute-start | bytes 49160 | tf_op jit(solution)/shard_map/ppermute | solution.py:451
  8.5 5.0 %collective-permute-start.3 = (f32[32,128]{1,0:T(8,128)S(1)}, f32[32,128]{1,0:T(8,128)S(1)}, u32[]{:S(2)}, u32[]{:S(2)}) collective-permute-start(f32[32,128]{1,0:T(8,128)S(1)} %get-tuple-element.59), channel_id=1, source_target_pairs={{0,1},{1,0},{2,3},{3,2},{4,5},{5,4},{6,7},{7,6},{8,16},{9,17},{10,... | collective-permute-start | bytes 49160 | tf_op jit(solution)/shard_map/ppermute | solution.py:451
  13.6 0.0 copy-done
  13.6 0.0 copy-done.2
  13.6 0.0 copy-done.1
  13.6 0.7 %shard_map.121 = (f32[12,128,128]{2,1,0:T(8,128)S(1)}, f32[6,64,128]{2,1,0:T(8,128)S(1)}, f32[3,32,128]{2,1,0:T(8,128)S(1)}, f32[3,16,128]{2,1,0:T(8,128)S(1)}, ...) custom-call(f32[3,4,128,128]{3,2,1,0:T(8,128)S(1)} %get-tuple-element.33.x_ref, ...), custom_call_target="tpu_custom_call" | custom-call | flops 1000000000 | bytes 2023424 | tf_op jit(solution)/shard_map/pallas_call | solution.py:429
  14.3 1.0 %collective-permute-done.3.got_b_ref = f32[32,128]{1,0:T(8,128)S(1)} collective-permute-done((f32[32,128]{1,0:T(8,128)S(1)}, f32[32,128]{1,0:T(8,128)S(1)}, u32[]{:S(2)}, u32[]{:S(2)}) %collective-permute-start.3) | collective-permute-done | bytes 16416 | tf_op jit(solution)/shard_map/ppermute | solution.py:451
  15.3 0.0 collective-permute-done.4.got_a_ref
  15.3 0.0 collective-permute-done.2.got_e_ref
  15.3 1.3 %shard_map.122 = (f32[3,128,512]{2,1,0:T(8,128)}, f32[3,64,256]{2,1,0:T(8,128)}, f32[3,32,128]{2,1,0:T(8,128)}, f32[3,16,64]{2,1,0:T(8,128)}, f32[3,8,32]{2,1,0:T(8,128)}, /*index=5*/f32[3,4,16]{2,1,0:T(4,128)}) custom-call(f32[12,128,128]{2,1,0:T(8,128)S(1)} %get-tuple-element.52.g0, f32[6,64,128]{2,1,0:T(8,128)S(1)} %get-tuple-element.53.g1, ...), custom_call_target="tpu_custom_call" | custom-call | flops 100000000 | bytes 1646592 | tf_op jit(solution)/shard_map/pallas_call | solution.py:429
Async XLA Ops:
  2.2 3.9 %collective-permute-start = (f32[3,16,128]{2,1,0:T(8,128)S(1)}, f32[3,16,128]{2,1,0:T(8,128)S(1)}, u32[]{:S(2)}, u32[]{:S(2)}) collective-permute-start(f32[3,16,128]{2,1,0:T(8,128)S(1)} %get-tuple-element.41), channel_id=1, source_target_pairs={{0,8},{1,2},{2,1},{3,4},{4,3},{5,6},{6,5},{7,15},{8,0},{9,10},{10,... | collective-permute-start | bytes 73736 | tf_op jit(solution)/shard_map/ppermute | solution.py:451
  4.2 1.9 %collective-permute-start.1 = (f32[3,16,128]{2,1,0:T(8,128)S(1)}, f32[3,16,128]{2,1,0:T(8,128)S(1)}, u32[]{:S(2)}, u32[]{:S(2)}) collective-permute-start(f32[3,16,128]{2,1,0:T(8,128)S(1)} %get-tuple-element.42), channel_id=1, source_target_pairs={{0,1},{1,0},{2,3},{3,2},{4,5},{5,4},{6,7},{7,6},{8,9},{9,8},{10,11... | collective-permute-start | bytes 73736 | tf_op jit(solution)/shard_map/ppermute | solution.py:451
  4.2 9.4 %copy-start = (bf16[256,512]{1,0:T(8,128)(2,1)S(1)}, bf16[256,512]{1,0:T(8,128)(2,1)}, u32[]{:S(2)}) copy-start(bf16[256,512]{1,0:T(8,128)(2,1)} %constant.15.clone.e0) | copy-start | bytes 786436
  4.2 9.4 %copy-start.2 = (bf16[128,384]{1,0:T(8,128)(2,1)S(1)}, bf16[128,384]{1,0:T(8,128)(2,1)}, u32[]{:S(2)}) copy-start(bf16[128,384]{1,0:T(8,128)(2,1)} %constant.17.clone.e2) | copy-start | bytes 294916
  5.5 8.0 %copy-start.1 = (bf16[256,256]{1,0:T(8,128)(2,1)S(1)}, bf16[256,256]{1,0:T(8,128)(2,1)}, u32[]{:S(2)}) copy-start(bf16[256,256]{1,0:T(8,128)(2,1)} %constant.16.clone.e1) | copy-start | bytes 393220
  6.4 8.9 %collective-permute-start.4 = (f32[32,128]{1,0:T(8,128)S(1)}, f32[32,128]{1,0:T(8,128)S(1)}, u32[]{:S(2)}, u32[]{:S(2)}) collective-permute-start(f32[32,128]{1,0:T(8,128)S(1)} %get-tuple-element.58), channel_id=1, source_target_pairs={{0,8},{1,9},{2,10},{3,11},{4,12},{5,13},{6,14},{7,15},{8,0},{9,1},... | collective-permute-start | bytes 49160 | tf_op jit(solution)/shard_map/ppermute | solution.py:451
  6.5 8.8 %collective-permute-start.2 = (f32[32,128]{1,0:T(8,128)S(1)}, f32[32,128]{1,0:T(8,128)S(1)}, u32[]{:S(2)}, u32[]{:S(2)}) collective-permute-start(f32[32,128]{1,0:T(8,128)S(1)} %get-tuple-element.58), channel_id=1, source_target_pairs={{0,1},{1,0},{2,3},{3,2},{4,5},{5,4},{6,7},{7,6},{8,9},{9,8},{10,11... | collective-permute-start | bytes 49160 | tf_op jit(solution)/shard_map/ppermute | solution.py:451
  8.5 6.7 %collective-permute-start.3 = (f32[32,128]{1,0:T(8,128)S(1)}, f32[32,128]{1,0:T(8,128)S(1)}, u32[]{:S(2)}, u32[]{:S(2)}) collective-permute-start(f32[32,128]{1,0:T(8,128)S(1)} %get-tuple-element.59), channel_id=1, source_target_pairs={{0,1},{1,0},{2,3},{3,2},{4,5},{5,4},{6,7},{7,6},{8,16},{9,17},{10,... | collective-permute-start | bytes 49160 | tf_op jit(solution)/shard_map/ppermute | solution.py:451
